TPU v7x, 32 devices: a whole 2x2x4 slice. The times are simulated.
32 devices in a mesh: grid: 4 (over z), line: 8 (over y, x, core).
Axes of the slice: x: 2, y: 2, z: 4, core: 2. Of those that a mesh axis runs over, the one named last changes fastest.
Arguments:
- les: float32 [24, 4, 1024], P(None, 'grid', 'line'), may hold values from -6 to 6
- lines: float32 [4, 8, 128, 24, 128], P('grid', 'line'), may hold values from -6 to 6
- triplet_start: int32 [2, 4, 8, 128], P(None, 'grid', 'line'), may hold values from 0 to 80
- splice_owner: int32 [2, 4, 8, 128, 1], P(None, 'grid', 'line'), may hold values from 0 to 31; in each aligned block of 128 rows (0 to 127, 128 to 255, ..., all dimensions but the last counted through in order) at most 8 rows name the same one
- splice_line: int32 [2, 4, 8, 128], P(None, 'grid', 'line'), may hold values from 0 to 127
- splice_from: int32 [2, 4, 8, 128], P(None, 'grid', 'line'), may hold values from 0 to 7
- splice_to: int32 [2, 4, 8, 128], P(None, 'grid', 'line'), may hold values from 0 to 7
- chem_counts: int32 [4, 8, 128], P('grid', 'line'), may hold values from 1 to 6, as said below
- diffusivity: float32 [24], replicated, may hold values from 0.5 to 20
- rates: float32 [24, 24], replicated, may hold values from -1.25 to 1.25
- frozen_inverse: float32 [24, 24], replicated, may hold values from -0.3 to 0.5
Outputs:
- les_out: float32 [24, 4, 1024], P(None, 'grid', 'line')
- lines_out: float32 [4, 8, 128, 24, 128], P('grid', 'line')
Inputs may be any that keep to these rules, and one draw needn't show every extreme that they name: `splice_owner`: in the rows of one device and one step no owner is named more than 8 times, a bound that some block reaches. `chem_counts`: some line has 6 substeps.
All inputs are finite; a program needn't handle non-finite values.
Results may differ from a plain program's by a relative error of at most 0.0003.
Values sent between devices are 32-bit elements; how exact they have to be, the bound alone decides.
A program may use at most 64 MiB of HBM per device.

v0:
```python
import functools

import jax
import jax.numpy as jnp
from jax import lax
from jax.experimental import pallas as pl
from jax.experimental.pallas import tpu as pltpu
from jax.sharding import PartitionSpec as P

SEG = 16
TRIP = 48
STEPS = 2

les_rate = 0.2
relax_rate = 0.5
splice_weight = 0.5

VMEM = pl.BlockSpec(memory_space=pltpu.VMEM)
SMEM = pl.BlockSpec(memory_space=pltpu.SMEM)


def rim_kernel(names, x_ref, o_ref, send_sem, recv_sem):
    at = [lax.axis_index(n) for n in names]
    size = [lax.axis_size(n) for n in names]
    devices = []
    for axis in (0, 1):
        for move in (1, size[axis] - 1):
            there = list(at)
            there[axis] = lax.rem(at[axis] + move, size[axis])
            devices.append(tuple(there))
    barrier = pltpu.get_barrier_semaphore()
    for device in devices:
        pl.semaphore_signal(barrier, inc=1, device_id=device, device_id_type=pl.DeviceIdType.MESH)
    pl.semaphore_wait(barrier, 4)
    copies = [
        pltpu.make_async_remote_copy(
            src_ref=x_ref,
            dst_ref=o_ref.at[k],
            send_sem=send_sem.at[k],
            recv_sem=recv_sem.at[k],
            device_id=devices[k],
            device_id_type=pl.DeviceIdType.MESH,
        )
        for k in range(4)
    ]
    for copy in copies:
        copy.start()
    for copy in copies:
        copy.wait()


def neighbours(field, number):
    species, cx, cy = field.shape
    flat = field.reshape(species, cx * cy)
    names = ("grid", "line")
    got = pl.pallas_call(
        functools.partial(rim_kernel, names),
        out_shape=jax.ShapeDtypeStruct((4,) + flat.shape, flat.dtype),
        in_specs=[VMEM],
        out_specs=VMEM,
        scratch_shapes=[pltpu.SemaphoreType.DMA((4,)), pltpu.SemaphoreType.DMA((4,))],
        compiler_params=pltpu.CompilerParams(collective_id=number, has_side_effects=True),
        name="rim%d" % number,
    )(flat).reshape((4,) + field.shape)
    total = 0.0
    for axis, dim in (("grid", 1), ("line", 2)):
        peers, length, at = lax.axis_size(axis), field.shape[dim], lax.axis_index(axis)
        before = lax.slice_in_dim(got[2 * dim - 2], length - 1, length, axis=dim)
        after = lax.slice_in_dim(got[2 * dim - 1], 0, 1, axis=dim)
        before = jnp.where(at > 0, before, 0.0)
        after = jnp.where(at < peers - 1, after, 0.0)
        total += jnp.concatenate([before, lax.slice_in_dim(field, 0, length - 1, axis=dim)], axis=dim)
        total += jnp.concatenate([lax.slice_in_dim(field, 1, length, axis=dim), after], axis=dim)
    return total


def diffusion_inverse(diffusivity, points):
    coeff = diffusivity[:, None]
    root = jnp.sqrt(4.0 * coeff + 1.0)
    theta = -jnp.log(2.0 * coeff / (2.0 * coeff + 1.0 + root))
    place = jnp.arange(points, dtype=jnp.float32)
    low = 1.0 + jnp.exp(-(2.0 * place + 1.0)[None, :] * theta)
    high = 1.0 + jnp.exp(-(2.0 * (points - place) - 1.0)[None, :] * theta)
    scale = 1.0 / (root * (1.0 - jnp.exp(-2.0 * points * theta)))
    apart = jnp.abs(place[:, None] - place[None, :])
    ends = jnp.where(
        (place[:, None] <= place[None, :])[None],
        low[:, :, None] * high[:, None, :],
        low[:, None, :] * high[:, :, None],
    )
    return jnp.exp(-apart[None] * theta[:, :, None]) * ends * scale[:, :, None]


def halves(value):
    top = value.astype(jnp.bfloat16)
    return top, (value - top.astype(jnp.float32)).astype(jnp.bfloat16)


def diffuse_kernel(species, x_ref, start_ref, m_ref, o_ref):
    points = x_ref.shape[1]
    lines = x_ref.shape[0] // species
    start = start_ref[...]
    place = lax.broadcasted_iota(jnp.int32, (lines, points), 1)
    rel = place - start
    third = TRIP // 3
    source = jnp.where(
        rel < third,
        3 * rel,
        jnp.where(rel < 2 * third, 3 * (2 * third - 1 - rel) + 1, 3 * (rel - 2 * third) + 2),
    )
    index = jnp.where((rel >= 0) & (rel < TRIP), source + start, place)

    def one(s, carry):
        y = x_ref[pl.ds(s, lines, stride=species), :]
        y = jnp.take_along_axis(y, index, axis=1, mode="promise_in_bounds")
        top, rest = halves(y)
        mtop, mrest = halves(m_ref[s])
        dot = functools.partial(jnp.dot, preferred_element_type=jnp.float32)
        out = dot(top, mtop) + dot(rest, mtop) + dot(top, mrest)
        o_ref[pl.ds(s, lines, stride=species), :] = out
        return carry

    lax.fori_loop(0, species, one, 0, unroll=4)


def chem_kernel(chunk, y_ref, mid_ref, a_ref, turns_ref, counts_ref, owner_ref, rank_ref, from_ref, o_ref, send_ref, other_ref):
    lines, species, points = y_ref.shape
    lane = lax.broadcasted_iota(jnp.int32, (species, points), 1)
    send_ref[...] = jnp.zeros_like(send_ref)
    mid = mid_ref[...]

    def lift(l, carry):
        add = jnp.take_along_axis(mid, jnp.full((species, points), l, jnp.int32), axis=1, mode="promise_in_bounds")
        o_ref[l] = y_ref[l] + relax_rate * add
        return carry

    lax.fori_loop(0, lines, lift, 0, unroll=8)
    matrix = a_ref[...]

    def substep(sub, in_ref, out_ref):
        def part(c, inner):
            base = c * chunk
            for q in range(0, chunk, 4):
                columns = []
                state = []
                for h in (0, 2):
                    y = in_ref[pl.ds(base + q + h, 2)].reshape(2 * species, points)
                    state.append(y)
                    top, rest = halves(jnp.tanh(y))
                    columns.append(jnp.concatenate([top, top, rest], axis=0))
                right = jnp.concatenate(columns, axis=1)
                change = jnp.dot(matrix, right, preferred_element_type=jnp.float32)
                for h in (0, 1):
                    for k in (0, 1):
                        l = base + q + 2 * h + k
                        factor = jnp.where(counts_ref[l] > sub, jnp.float32(1.0), jnp.float32(0.0))
                        rows = slice(k * species, (k + 1) * species)
                        out_ref[l] = state[h][rows] + factor * change[rows, h * points : (h + 1) * points]
            return inner

        lax.fori_loop(0, lines // chunk, part, 0)

    def two(pair, carry):
        substep(2 * pair, o_ref, other_ref)
        substep(2 * pair + 1, other_ref, o_ref)
        return carry

    lax.fori_loop(0, (turns_ref[0] + 1) // 2, two, 0)

    def pack(l, carry):
        slot = rank_ref[l]
        owner = owner_ref[l]
        move = (SEG * (slot - from_ref[l])) & (points - 1)
        value = pltpu.roll(o_ref[l], move, 1)
        send_ref[owner] = jnp.where(lane // SEG == slot, value, send_ref[owner])
        return carry

    lax.fori_loop(0, lines, pack, 0, unroll=8)


def swap_kernel(names, groups, pairs, *refs):
    sends, takes = refs[:pairs], refs[pairs : 2 * pairs]
    send_sem, recv_sem, own_sem = refs[2 * pairs :]
    width = lax.axis_size(names[1])
    me = lax.axis_index(names[0]) * width + lax.axis_index(names[1])

    def place(j):
        peer = lax.rem(me + j, groups)
        return peer, (peer // width, lax.rem(peer, width))

    barrier = pltpu.get_barrier_semaphore()

    def greet(j, carry):
        pl.semaphore_signal(barrier, inc=1, device_id=place(j)[1], device_id_type=pl.DeviceIdType.MESH)
        return carry

    lax.fori_loop(1, groups, greet, 0)
    own = [pltpu.make_async_copy(sends[p].at[me], takes[p].at[me], own_sem.at[p]) for p in range(pairs)]
    for copy in own:
        copy.start()
    pl.semaphore_wait(barrier, groups - 1)

    def copies(j):
        peer, device = place(j)
        return [
            pltpu.make_async_remote_copy(
                src_ref=sends[p].at[peer],
                dst_ref=takes[p].at[me],
                send_sem=send_sem.at[p, j],
                recv_sem=recv_sem.at[p, j],
                device_id=device,
                device_id_type=pl.DeviceIdType.MESH,
            )
            for p in range(pairs)
        ]

    def begin(j, carry):
        for copy in copies(j):
            copy.start()
        return carry

    def finish(j, carry):
        for copy in copies(j):
            copy.wait()
        return carry

    lax.fori_loop(1, groups, begin, 0)
    for copy in own:
        copy.wait()
    lax.fori_loop(1, groups, finish, 0)


def swap(arrays, number):
    names = ("grid", "line")
    groups = arrays[0].shape[0]
    pairs = len(arrays)
    return pl.pallas_call(
        functools.partial(swap_kernel, names, groups, pairs),
        out_shape=[jax.ShapeDtypeStruct(a.shape, a.dtype) for a in arrays],
        in_specs=[VMEM] * pairs,
        out_specs=[VMEM] * pairs,
        scratch_shapes=[
            pltpu.SemaphoreType.DMA((pairs, groups)),
            pltpu.SemaphoreType.DMA((pairs, groups)),
            pltpu.SemaphoreType.DMA((pairs,)),
        ],
        compiler_params=pltpu.CompilerParams(collective_id=number, has_side_effects=True),
        name="swap%d" % number,
    )(*arrays)


def land_kernel(step, slots, y_ref, recv_ref, aim_ref, mid_ref, o_ref, les_ref):
    lines, species, points = y_ref.shape
    groups = recv_ref.shape[0]
    segments = points // SEG
    lane = lax.broadcasted_iota(jnp.int32, (species, points), 1)
    o_ref[...] = y_ref[...]

    def land(r, carry):
        got = recv_ref[r]
        for k in range(slots):
            code = aim_ref[r, 0, step * slots + k]
            safe = jnp.maximum(code, 0)
            line = safe // segments
            seg = safe - line * segments
            value = pltpu.roll(got, (SEG * (seg - k)) & (points - 1), 1)
            hit = lane // SEG == jnp.where(code >= 0, seg, -1)
            o_ref[line] = o_ref[line] + jnp.where(hit, splice_weight * (value - y_ref[line]), 0.0)
        return carry

    lax.fori_loop(0, groups, land, 0)

    def filtered(l, total):
        return jnp.where(lane == l, jnp.sum(o_ref[l], axis=1, keepdims=True), total)

    total = lax.fori_loop(0, lines, filtered, jnp.zeros((species, points), jnp.float32), unroll=8)
    les_ref[...] = 0.5 * mid_ref[...] + (0.5 / points) * total


def body(
    les,
    lines,
    triplet_start,
    splice_owner,
    splice_line,
    splice_from,
    splice_to,
    chem_counts,
    diffusivity,
    rates,
    frozen_inverse,
):
    groups = lax.axis_size("grid") * lax.axis_size("line")
    _, _, count, species, points = lines.shape
    segments = points // SEG
    slots = min(segments, max(2, 2 * count // groups))
    f32 = jnp.float32
    params = pltpu.CompilerParams(vmem_limit_bytes=40 * 1024 * 1024)

    mixing = diffusion_inverse(diffusivity, points) - relax_rate / points
    joint = jnp.dot(frozen_inverse, rates, precision=lax.Precision.HIGHEST)
    twice = jnp.kron(jnp.eye(2, dtype=f32), joint)
    top = lax.reduce_precision(twice, 8, 7)
    rest = lax.reduce_precision(twice - top, 8, 7)
    matrix = jnp.concatenate([top, rest, top], axis=1).astype(jnp.bfloat16)

    starts = triplet_start.reshape(STEPS, count, 1)
    owner = splice_owner.reshape(STEPS, count)
    line_to = splice_line.reshape(STEPS, count)
    seg_from = splice_from.reshape(STEPS, count)
    seg_to = splice_to.reshape(STEPS, count)
    counts = chem_counts.reshape(count)
    turns = jnp.max(counts).reshape(1)
    order = jnp.arange(count)
    earlier = (owner[:, :, None] == owner[:, None, :]) & (order[None, :, None] > order[None, None, :])
    rank = jnp.sum(earlier.astype(jnp.int32), axis=2)
    position = owner * slots + rank
    code = line_to * segments + seg_to
    hit = jnp.arange(groups * slots)[None, :, None] == position[:, None, :]
    aims = jnp.max(jnp.where(hit, code[:, None, :], -1), axis=2)
    aims = aims.reshape(STEPS, groups, slots).transpose(1, 0, 2).reshape(groups, 1, STEPS * slots)
    aims = jnp.pad(aims, ((0, 0), (0, 0), (0, points - STEPS * slots)))

    diffuse = pl.pallas_call(
        functools.partial(diffuse_kernel, species),
        out_shape=jax.ShapeDtypeStruct((count * species, points), f32),
        in_specs=[VMEM] * 3,
        out_specs=VMEM,
        compiler_params=params,
        cost_estimate=pl.CostEstimate(flops=6 * species * count * points * points, bytes_accessed=5 << 20, transcendentals=0),
        name="diffuse",
    )
    block = jax.ShapeDtypeStruct((count, species, points), f32)
    chem = pl.pallas_call(
        functools.partial(chem_kernel, 64),
        out_shape=(block, jax.ShapeDtypeStruct((groups, species, points), f32)),
        in_specs=[VMEM] * 3 + [SMEM] * 5,
        out_specs=(VMEM, VMEM),
        scratch_shapes=[pltpu.VMEM((count, species, points), f32)],
        compiler_params=params,
        name="chem",
    )
    def land(step, *given):
        return pl.pallas_call(
            functools.partial(land_kernel, step, slots),
            out_shape=(block, jax.ShapeDtypeStruct((species, count), f32)),
            in_specs=[VMEM, VMEM, SMEM, VMEM],
            out_specs=(VMEM, VMEM),
            compiler_params=params,
            name="land",
        )(*given)

    field = les
    state = lines.reshape(count, species, points)
    for step in range(STEPS):
        beside = neighbours(field, STEPS + step)
        mid = (field + les_rate * (beside - 4.0 * field)).reshape(species, count)
        spread = diffuse(state.reshape(count * species, points), starts[step], mixing)
        state, sending = chem(
            spread.reshape(count, species, points), mid, matrix, turns, counts, owner[step], rank[step], seg_from[step]
        )
        if step == 0:
            received, aims = swap([sending, aims], 0)
        else:
            (received,) = swap([sending], step)
        state, field = land(step, state, received, aims, mid)
        field = field.reshape(les.shape)
    return (field, state.reshape(lines.shape))


def solution(mesh):
    in_specs = (
        P(None, "grid", "line"),
        P("grid", "line", None, None, None),
        P(None, "grid", "line", None),
        P(None, "grid", "line", None, None),
        P(None, "grid", "line", None),
        P(None, "grid", "line", None),
        P(None, "grid", "line", None),
        P("grid", "line", None),
        P(),
        P(),
        P(),
    )
    out_specs = (P(None, "grid", "line"), P("grid", "line", None, None, None))
    return jax.shard_map(body, mesh=mesh, in_specs=in_specs, out_specs=out_specs, check_vma=False)
```

profile of v0, /device:TPU:0, one launch (start us, length us, event | category | flops | bytes accessed | tf_op | source)
XLA Modules:
  0.0 103.0 jit_solution(13419639217738833031)
XLA Ops:
  0.7 10.0 %rim2.1 = f32[4,24,128]{2,1,0:T(8,128)} custom-call(f32[24,128]{1,0:T(8,128)} %bitcast.67), custom_call_target="tpu_custom_call" | custom-call | tf_op jit(solution)/shard_map/rim2/pallas_call | solution.py:56
  10.7 0.7 slice_bitcast_fusion.4
  11.5 0.9 fusion.13
  12.4 0.8 fusion.8.mid_ref
  14.1 1.0 multiply_add_fusion.m_ref
  15.2 1.4 %copy-done.1 = f32[1,1,128,24,128]{4,3,2,1,0:T(8,128)S(1)} copy-done((f32[1,1,128,24,128]{4,3,2,1,0:T(8,128)S(1)}, f32[1,1,128,24,128]{4,3,2,1,0:T(8,128)}, u32[]{:S(2)}) %copy-start.1) | copy-done | bytes 1572888
  16.6 2.6 %diffuse.2 = f32[3072,128]{1,0:T(8,128)S(1)} custom-call(f32[3072,128]{1,0:T(8,128)S(1)} %bitcast.62, s32[128,1]{1,0:T(8,128)S(1)} %copy.33.start_ref, f32[24,128,128]{2,1,0:T(8,128)S(1)} %multiply_add_fusion.m_ref), custom_call_target="tpu_custom_call" | custom-call | flops 301989888 | bytes 5242880 | tf_op jit(solution)/shard_map/diffuse/pallas_call | solution.py:358
  20.6 8.6 %chem.2 = (f32[128,24,128]{2,1,0:T(8,128)S(1)}, f32[32,24,128]{2,1,0:T(8,128)S(1)}) custom-call(f32[128,24,128]{2,1,0:T(8,128)S(1)} %bitcast.60, f32[24,128]{1,0:T(8,128)S(1)} %fusion.8.mid_ref, bf16[48,144]{1,0:T(8,128)(2,1)S(1)} %pad_maximum_fusion.a_ref, s32[1]{0:T(128)} %bitcast.12.turns_ref, s32[128]{0:T(128)S(1)} %bitcast.65, ...), custom_call_target="tpu_custom_call" | custom-call | tf_op jit(solution)/shard_map/chem/pallas_call | solution.py:359
  29.2 1.1 %copy-done.2 = f32[128,24,128]{2,1,0:T(8,128)} copy-done((f32[128,24,128]{2,1,0:T(8,128)}, f32[128,24,128]{2,1,0:T(8,128)S(1)}, u32[]{:S(2)}) %copy-start.2) | copy-done | bytes 1572888
  30.3 0.7 copy-done.5
  32.1 14.0 %swap0.1 = (f32[32,24,128]{2,1,0:T(8,128)}, s32[32,1,128]{2,1,0:T(1,128)}) custom-call(f32[32,24,128]{2,1,0:T(8,128)} %copy-done.5, s32[32,1,128]{2,1,0:T(1,128)} %pad.4.refs_1_), custom_call_target="tpu_custom_call" | custom-call | tf_op jit(solution)/shard_map/swap0/pallas_call | solution.py:237
  46.1 1.4 %copy-done.3 = f32[128,24,128]{2,1,0:T(8,128)S(1)} copy-done((f32[128,24,128]{2,1,0:T(8,128)S(1)}, f32[128,24,128]{2,1,0:T(8,128)}, u32[]{:S(2)}) %copy-start.3) | copy-done | bytes 1572888
  47.5 1.0 copy-done.7
  49.3 6.4 %land.2 = (f32[128,24,128]{2,1,0:T(8,128)S(1)}, f32[24,128]{1,0:T(8,128)S(1)}) custom-call(f32[128,24,128]{2,1,0:T(8,128)S(1)} %copy-done.3, f32[32,24,128]{2,1,0:T(8,128)S(1)} %copy-done.7, s32[32,1,128]{2,1,0:T(1,128)S(1)} %copy-done.9, f32[24,128]{1,0:T(8,128)S(1)} %fusion.8.mid_ref), custom_call_target="tpu_custom_call" | custom-call | tf_op jit(solution)/shard_map/land/pallas_call | solution.py:344
  56.3 10.7 %rim3.1 = f32[4,24,128]{2,1,0:T(8,128)} custom-call(f32[24,128]{1,0:T(8,128)} %copy-done.8), custom_call_target="tpu_custom_call" | custom-call | tf_op jit(solution)/shard_map/rim3/pallas_call | solution.py:56
  67.0 0.7 slice_bitcast_fusion.2
  67.8 0.9 slice_bitcast_fusion
  68.7 0.8 fusion.12.mid_ref
  69.6 2.6 %diffuse.3 = f32[3072,128]{1,0:T(8,128)S(1)} custom-call(f32[3072,128]{1,0:T(8,128)S(1)} %bitcast.63, s32[128,1]{1,0:T(8,128)S(1)} %copy.40.start_ref, f32[24,128,128]{2,1,0:T(8,128)S(1)} %multiply_add_fusion.m_ref), custom_call_target="tpu_custom_call" | custom-call | flops 301989888 | bytes 5242880 | tf_op jit(solution)/shard_map/diffuse/pallas_call | solution.py:358
  72.2 8.6 %chem.3 = (f32[128,24,128]{2,1,0:T(8,128)S(1)}, f32[32,24,128]{2,1,0:T(8,128)S(1)}) custom-call(f32[128,24,128]{2,1,0:T(8,128)S(1)} %bitcast.61, f32[24,128]{1,0:T(8,128)S(1)} %fusion.12.mid_ref, bf16[48,144]{1,0:T(8,128)(2,1)S(1)} %pad_maximum_fusion.a_ref, s32[1]{0:T(128)} %bitcast.12.turns_ref, s32[128]{0:T(128)S(1)} %bitcast.66, ...), custom_call_target="tpu_custom_call" | custom-call | tf_op jit(solution)/shard_map/chem/pallas_call | solution.py:359
  80.8 0.7 copy-done.6
  81.5 13.0 %swap1.1.recv_ref = f32[32,24,128]{2,1,0:T(8,128)} custom-call(f32[32,24,128]{2,1,0:T(8,128)} %copy-done.6), custom_call_target="tpu_custom_call" | custom-call | tf_op jit(solution)/shard_map/swap1/pallas_call | solution.py:237
  94.5 1.0 copy-done.4
  95.5 7.5 %land.3 = (f32[128,24,128]{2,1,0:T(8,128)}, f32[24,128]{1,0:T(8,128)}) custom-call(f32[128,24,128]{2,1,0:T(8,128)S(1)} %get-tuple-element.18.y_ref, f32[32,24,128]{2,1,0:T(8,128)S(1)} %copy-done.4, s32[32,1,128]{2,1,0:T(1,128)S(1)} %copy-done.10, f32[24,128]{1,0:T(8,128)S(1)} %fusion.12.mid_ref), custom_call_target="tpu_custom_call" | custom-call | tf_op jit(solution)/shard_map/land/pallas_call | solution.py:344
  (59 shorter events, 4.9 us)
Async XLA Ops:
  0.6 18.6 %copy-start = (f32[24,24]{1,0:T(8,128)S(1)}, f32[24,24]{1,0:T(8,128)}, u32[]{:S(2)}) copy-start(f32[24,24]{1,0:T(8,128)} %param.21) | copy-start | bytes 6916
  0.6 14.4 %copy-start.16 = (s32[2,1,1,128]{3,2,1,0:T(1,128)S(1)}, s32[2,1,1,128]{3,2,1,0:T(1,128)}, u32[]{:S(2)}) copy-start(s32[2,1,1,128]{3,2,1,0:T(1,128)} %param.13) | copy-start | bytes 3076
  15.2 1.4 %copy-start.1 = (f32[1,1,128,24,128]{4,3,2,1,0:T(8,128)S(1)}, f32[1,1,128,24,128]{4,3,2,1,0:T(8,128)}, u32[]{:S(2)}) copy-start(f32[1,1,128,24,128]{4,3,2,1,0:T(8,128)} %param.12) | copy-start | bytes 4718596
  16.6 2.6 %copy-start.13 = (f32[24,24]{1,0:T(8,128)S(1)}, f32[24,24]{1,0:T(8,128)}, u32[]{:S(2)}) copy-start(f32[24,24]{1,0:T(8,128)} %param.20) | copy-start | bytes 6916
  16.6 3.1 %copy-start.12 = (s32[2,1,1,128,1]{3,4,2,1,0:T(1,128)S(1)}, s32[2,1,1,128,1]{3,4,2,1,0:T(1,128)}, u32[]{:S(2)}) copy-start(s32[2,1,1,128,1]{3,4,2,1,0:T(1,128)} %param.14) | copy-start | bytes 3076
  16.6 3.3 %copy-start.17 = (s32[2,1,1,128]{3,2,1,0:T(1,128)S(1)}, s32[2,1,1,128]{3,2,1,0:T(1,128)}, u32[]{:S(2)}) copy-start(s32[2,1,1,128]{3,2,1,0:T(1,128)} %param.16) | copy-start | bytes 3076
  16.6 3.3 %copy-start.11 = (s32[1,1,128]{2,1,0:T(1,128)S(1)}, s32[1,1,128]{2,1,0:T(1,128)}, u32[]{:S(2)}) copy-start(s32[1,1,128]{2,1,0:T(1,128)} %param.18) | copy-start | bytes 1540
  19.2 11.9 %copy-start.14 = (s32[2,1,1,128]{3,2,1,0:T(1,128)S(1)}, s32[2,1,1,128]{3,2,1,0:T(1,128)}, u32[]{:S(2)}) copy-start(s32[2,1,1,128]{3,2,1,0:T(1,128)} %param.17) | copy-start | bytes 3076
  19.2 11.8 %copy-start.15 = (s32[2,1,1,128]{3,2,1,0:T(1,128)S(1)}, s32[2,1,1,128]{3,2,1,0:T(1,128)}, u32[]{:S(2)}) copy-start(s32[2,1,1,128]{3,2,1,0:T(1,128)} %param.15) | copy-start | bytes 3076
  29.2 1.1 %copy-start.2 = (f32[128,24,128]{2,1,0:T(8,128)}, f32[128,24,128]{2,1,0:T(8,128)S(1)}, u32[]{:S(2)}) copy-start(f32[128,24,128]{2,1,0:T(8,128)S(1)} %get-tuple-element.12.y_ref) | copy-start | bytes 4718596
  30.3 0.7 copy-start.5
  46.1 1.4 %copy-start.3 = (f32[128,24,128]{2,1,0:T(8,128)S(1)}, f32[128,24,128]{2,1,0:T(8,128)}, u32[]{:S(2)}) copy-start(f32[128,24,128]{2,1,0:T(8,128)} %copy-done.2) | copy-start | bytes 4718596
  47.5 1.0 copy-start.7
  48.5 0.7 copy-start.9
  55.7 0.6 copy-start.8
  72.2 22.3 %copy-start.10 = (s32[32,1,128]{2,1,0:T(1,128)S(1)}, s32[32,1,128]{2,1,0:T(1,128)}, u32[]{:S(2)}) copy-start(s32[32,1,128]{2,1,0:T(1,128)} %get-tuple-element.15.aim_ref) | copy-start | bytes 49156
  80.7 0.7 copy-start.6
  94.5 1.0 copy-start.4
where the time goes:
time: 105 us; the launch traced here: 103 us
  Pallas kernels  83.9 us (80%)
  local copies, waits for them, and re-layouts  13.1 us (12%)
  other arithmetic  4.84 us (5%)
    pallas_call x2, Pallas kernels, swap(): pl.pallas_call(functools.partial(swap_kernel, names, groups, pairs), out_...  27 us
    pallas_call x2, Pallas kernels, neighbours(): pl.pallas_call(functools.partial(rim_kernel, names), out_shape=jax.ShapeD...  20.7 us
    pallas_call x2, Pallas kernels, body(): chem(spread.reshape(count, species, points), mid, matrix, turns, counts,...  17.1 us
    pallas_call x2, Pallas kernels, land(): pl.pallas_call(functools.partial(land_kernel, step, slots), out_shape=(bl...  13.9 us
    unnamed x36, local copies, waits for them, and re-layouts  8.77 us
    pallas_call x2, Pallas kernels, body(): diffuse(state.reshape(count * species, points), starts[step], mixing)  5.11 us

commit v1 on v0

v1 whole, which is shorter than its diff:
```python
import functools

import jax
import jax.numpy as jnp
from jax import lax
from jax.experimental import pallas as pl
from jax.experimental.pallas import tpu as pltpu
from jax.sharding import PartitionSpec as P

SEG = 16
TRIP = 48
STEPS = 2
SUBSTEPS = 6

les_rate = 0.2
relax_rate = 0.5
splice_weight = 0.5

NAMES = ("grid", "line")
MESH = pl.DeviceIdType.MESH
VMEM = pl.BlockSpec(memory_space=pltpu.VMEM)
SMEM = pl.BlockSpec(memory_space=pltpu.SMEM)
ANY = pl.BlockSpec(memory_space=pl.ANY)
f32 = jnp.float32
bf16 = jnp.bfloat16
i32 = jnp.int32

dot = functools.partial(jnp.dot, preferred_element_type=jnp.float32)


def halves(value):
    top = value.astype(bf16)
    return top, (value - top.astype(f32)).astype(bf16)


def column(row):
    points = row.shape[1]
    return jnp.transpose(jnp.broadcast_to(row, (points, points)))


def iota(shape, axis):
    return lax.broadcasted_iota(i32, shape, axis)


def bits(size):
    assert size & (size - 1) == 0
    return size.bit_length() - 1


def when(condition, value):
    return jnp.where(condition, value, 0)


def total_of(value, axis):
    return jnp.sum(value, axis=axis, keepdims=True, dtype=i32)


def kernel(
    slots,
    les_ref,
    lines_ref,
    start_ref,
    owner_ref,
    line_ref,
    from_ref,
    to_ref,
    matrix_ref,
    coeff_ref,
    counts_ref,
    les_out,
    lines_out,
    y_ref,
    z_ref,
    m_top,
    m_rest,
    send_ref,
    recv_0,
    recv_1,
    sums_ref,
    weight_ref,
    rim_ref,
    field_ref,
    mid_ref,
    aim_ref,
    got_ref,
    flat_ref,
    tab_ref,
    tab_smem,
    load_sem,
    tab_sem,
    rim_send,
    rim_recv,
    aim_send,
    aim_recv,
    send_sem,
    recv_sem,
    out_sem,
):
    species, lines = les_ref.shape
    points = y_ref.shape[2]
    segments = points // SEG
    size = [lax.axis_size(n) for n in NAMES]
    at = [lax.axis_index(n) for n in NAMES]
    groups = size[0] * size[1]
    me = at[0] * size[1] + at[1]
    total = groups * slots
    blocks = total // points
    recv_refs = (recv_0, recv_1)

    def place(j):
        peer = lax.rem(me + j, groups)
        return peer, (peer // size[1], lax.rem(peer, size[1]))

    barrier = pltpu.get_barrier_semaphore()

    def greet(j, carry):
        pl.semaphore_signal(barrier, inc=1, device_id=place(j)[1], device_id_type=MESH)
        return carry

    lax.fori_loop(1, groups, greet, 0)
    load = pltpu.make_async_copy(lines_ref, y_ref, load_sem)
    load.start()

    rims = []
    for axis in (0, 1):
        for move in (1, size[axis] - 1):
            there = list(at)
            there[axis] = lax.rem(at[axis] + move, size[axis])
            rims.append(tuple(there))

    def rim_copies(step):
        return [
            pltpu.make_async_remote_copy(
                src_ref=field_ref.at[step],
                dst_ref=rim_ref.at[step, k],
                send_sem=rim_send.at[step, k],
                recv_sem=rim_recv.at[step, k],
                device_id=rims[k],
                device_id_type=MESH,
            )
            for k in range(4)
        ]

    def aim_copy(j):
        peer, device = place(j)
        return pltpu.make_async_remote_copy(
            src_ref=aim_ref.at[(peer * slots) // points],
            dst_ref=got_ref.at[me],
            send_sem=aim_send.at[j],
            recv_sem=aim_recv.at[j],
            device_id=device,
            device_id_type=MESH,
        )

    def data_copy(step, j):
        peer, device = place(j)
        return pltpu.make_async_remote_copy(
            src_ref=send_ref.at[step, peer],
            dst_ref=recv_refs[step].at[me],
            send_sem=send_sem.at[step, j],
            recv_sem=recv_sem.at[step, j],
            device_id=device,
            device_id_type=MESH,
        )

    field_ref[0] = les_ref[...]

    lane = iota((points, points), 1)
    row = iota((points, points), 0)
    for step in range(STEPS):
        owner = owner_ref[step : step + 1, :]
        rank = total_of(when((column(owner) == owner) & (row < lane), 1), 0)
        spot = column(owner * slots + rank)
        code = column(iota((1, points), 1) * segments + from_ref[step : step + 1, :])
        aim = column(line_ref[step : step + 1, :] * segments + to_ref[step : step + 1, :] + 1)
        for b in range(blocks):
            hit = spot == lane + b * points
            tab_ref[step * blocks + b] = total_of(when(hit, code), 0)
            aim_ref[b, step : step + 1, :] = total_of(when(hit, aim), 0)
    send_rows = STEPS * blocks
    send_table = pltpu.make_async_copy(tab_ref.at[pl.ds(0, send_rows)], tab_smem.at[pl.ds(0, send_rows)], tab_sem.at[0])
    send_table.start()

    apart = jnp.abs(lane - row).astype(f32)
    both = (lane + row).astype(f32)

    def inverse(s, carry):
        coeff = jnp.full((8, points), coeff_ref[s], f32)
        root = jnp.sqrt(4.0 * coeff + 1.0)
        theta = -jnp.log(2.0 * coeff / (2.0 * coeff + 1.0 + root))
        scale = 1.0 / (root * (1.0 - jnp.exp(-2.0 * points * theta)))
        theta = theta[:1]
        value = jnp.exp(-apart * theta) + jnp.exp((apart - 2.0 * points) * theta)
        value = value + jnp.exp(-(both + 1.0) * theta) + jnp.exp((both + 1.0 - 2.0 * points) * theta)
        top, rest = halves(value * scale[:1] - relax_rate / points)
        m_top[s] = top
        m_rest[s] = rest
        return carry

    lax.fori_loop(0, species, inverse, 0)

    pl.semaphore_wait(barrier, groups - 1)
    for copy in rim_copies(0):
        copy.start()

    def aim_start(j, carry):
        aim_copy(j).start()
        return carry

    lax.fori_loop(1, groups, aim_start, 0)
    got_ref[me] = aim_ref[(me * slots) // points]

    flat_y = y_ref.reshape(lines * species, points)
    flat_z = z_ref.reshape(lines * species, points)

    def diffuse(step):
        rel = lane - column(start_ref[step : step + 1, :])
        third = TRIP // 3
        source = jnp.where(
            rel < third,
            3 * rel,
            jnp.where(rel < 2 * third, 3 * (2 * third - 1 - rel) + 1, 3 * (rel - 2 * third) + 2),
        )
        index = jnp.where((rel >= 0) & (rel < TRIP), source + (lane - rel), lane)

        def one(s, carry):
            y = flat_y[pl.ds(s, lines, stride=species), :]
            y = jnp.take_along_axis(y, index, axis=1, mode="promise_in_bounds")
            top, rest = halves(y)
            out = dot(top, m_top[s]) + dot(rest, m_top[s]) + dot(top, m_rest[s])
            flat_z[pl.ds(s, lines, stride=species), :] = out
            return carry

        lax.fori_loop(0, species, one, 0, unroll=4)

    lane_s = lax.broadcasted_iota(i32, (species, points), 1)

    def middle(step):
        field = field_ref[step]
        up = jnp.where(at[0] > 0, rim_ref[step, 0], 0.0)
        down = jnp.where(at[0] < size[0] - 1, rim_ref[step, 1], 0.0)
        left = jnp.where(at[1] > 0, rim_ref[step, 2], 0.0)
        right = jnp.where(at[1] < size[1] - 1, rim_ref[step, 3], 0.0)
        before = pltpu.roll(jnp.where(lane_s == points - 1, left, field), 1, 1)
        after = pltpu.roll(jnp.where(lane_s == 0, right, field), points - 1, 1)
        mid_ref[...] = field + les_rate * (up + down + before + after - 4.0 * field)

    matrix = matrix_ref[...]
    chunk = 64

    def substep(sub, in_ref, out_ref, lift):
        def part(c, inner):
            base = c * chunk
            mid = mid_ref[...] if lift else None
            for q in range(0, chunk, 4):
                columns = []
                state = []
                for h in (0, 2):
                    y = in_ref[pl.ds(base + q + h, 2)].reshape(2 * species, points)
                    if lift:
                        add = [
                            jnp.take_along_axis(
                                mid, jnp.full((species, points), base + q + h + k, i32), axis=1, mode="promise_in_bounds"
                            )
                            for k in (0, 1)
                        ]
                        y = y + relax_rate * jnp.concatenate(add, axis=0)
                    state.append(y)
                    top, rest = halves(jnp.tanh(y))
                    columns.append(jnp.concatenate([top, top, rest], axis=0))
                right = jnp.concatenate(columns, axis=1)
                change = dot(matrix, right)
                for h in (0, 1):
                    for k in (0, 1):
                        l = base + q + 2 * h + k
                        factor = jnp.where(counts_ref[l] > sub, f32(1.0), f32(0.0))
                        rows = slice(k * species, (k + 1) * species)
                        value = state[h][rows] + factor * change[rows, h * points : (h + 1) * points]
                        out_ref[l] = value
            return inner

        lax.fori_loop(0, lines // chunk, part, 0)

    def chemistry():
        substep(0, z_ref, y_ref, True)

        def two(pair, carry):
            substep(2 * pair + 1, y_ref, z_ref, False)
            substep(2 * pair + 2, z_ref, y_ref, False)
            return carry

        lax.fori_loop(0, SUBSTEPS // 2 - 1, two, 0)
        substep(SUBSTEPS - 1, y_ref, z_ref, False)

    segment = lane_s // SEG

    def pack(step, peer):
        tile = jnp.zeros((species, points), f32)
        for k in range(slots):
            q = peer * slots + k
            code = tab_smem[step * blocks + q // points, 0, lax.rem(q, points)]
            value = z_ref[code >> bits(segments)]
            value = pltpu.roll(value, (SEG * (k - (code & (segments - 1)))) & (points - 1), 1)
            tile = jnp.where(segment == k, value, tile)
        return tile

    def exchange(step):
        def begin(j, carry):
            peer, _ = place(j)
            send_ref[step, peer] = pack(step, peer)

            @pl.when(j > 1)
            def _():
                data_copy(step, j - 1).start()

            return carry

        lax.fori_loop(1, groups, begin, 0)
        recv_refs[step][me] = pack(step, me)
        data_copy(step, groups - 1).start()

    def arrivals():
        number = iota((total, 1), 0)
        lane_t = iota((total, points), 1)
        number_r = iota((1, total), 1)
        offset = lax.rem(me * slots, points)
        mine = offset + (iota((total, points), 0) & (slots - 1))
        for step in range(STEPS):
            for r in range(groups):
                flat_ref[r * slots : (r + 1) * slots, :] = jnp.broadcast_to(
                    got_ref[r, step : step + 1, :], (slots, points)
                )
            code = total_of(when(lane_t == mine, flat_ref[...]), 1)
            valid = code > 0
            code = code - 1
            line = jnp.where(valid, code >> bits(segments), lines)
            seg = code & (segments - 1)
            line_c = jnp.broadcast_to(line, (total, points))
            line_r = jnp.concatenate(
                [jnp.transpose(line_c[b * points : (b + 1) * points])[:1] for b in range(blocks)], axis=1
            )
            key_r = line_r * total + number_r
            key_c = line * total + number
            below = key_r < key_c
            position = total_of(when(below, 1), 1)
            same = total_of(when(below & (line_r == line), 1), 1)
            value = (number * segments + seg) * 2 + when(same == 0, 1)
            base = send_rows + step * (blocks + 1)
            for b in range(blocks):
                tab_ref[base + b] = total_of(when(position == lane_t + b * points, value), 0)
            upto = total_of(when(line_c <= lane_t, 1), 0)
            many = total_of(when(line_c == lane_t, 1), 0)
            tab_ref[base + blocks] = jnp.maximum(upto - 1, 0) * 2 + when(many > 0, 1)
            lands = jnp.where(line_r == iota((lines, total), 0), 1.0, 0.0).astype(bf16)
            covers = jnp.where(seg == (lane_t >> bits(SEG)), 1.0, 0.0).astype(bf16)
            weight_ref[step] = 1.0 - splice_weight * dot(lands, covers)
        rows = STEPS * (blocks + 1)
        copy = pltpu.make_async_copy(
            tab_ref.at[pl.ds(send_rows, rows)], tab_smem.at[pl.ds(send_rows, rows)], tab_sem.at[1]
        )
        copy.start()
        copy.wait()

    def collect(step):
        def finish(j, carry):
            data_copy(step, j).wait()
            return carry

        lax.fori_loop(1, groups, finish, 0)

    def land(step):
        base = send_rows + step * (blocks + 1)

        def run(n, acc):
            code = tab_smem[base + n // points, 0, lax.rem(n, points)]
            first = code & 1
            seg = (code >> 1) & (segments - 1)
            number = code >> bits(2 * segments)
            source = number >> bits(slots)
            k = number & (slots - 1)
            value = pltpu.roll(recv_refs[step][source], (SEG * (seg - k)) & (points - 1), 1)
            value = jnp.where(segment == seg, value, 0.0)
            acc = value + jnp.where(first == 1, f32(0.0), f32(1.0)) * acc
            sums_ref[n] = acc
            return acc

        lax.fori_loop(0, total, run, jnp.zeros((species, points), f32), unroll=8)

        def settle(l, sums):
            code = tab_smem[base + blocks, 0, l]
            factor = jnp.where((code & 1) == 1, f32(splice_weight), f32(0.0))
            value = z_ref[l] * weight_ref[step, pl.ds(l, 1), :] + factor * sums_ref[code >> 1]
            y_ref[l] = value
            return jnp.where(lane_s == l, jnp.sum(value, axis=1, keepdims=True), sums)

        sums = lax.fori_loop(0, lines, settle, jnp.zeros((species, points), f32), unroll=8)
        return 0.5 * mid_ref[...] + (0.5 / points) * sums

    load.wait()
    diffuse(0)
    for copy in rim_copies(0):
        copy.wait()
    middle(0)
    send_table.wait()
    chemistry()
    exchange(0)

    def aim_finish(j, carry):
        aim_copy(j).wait()
        return carry

    lax.fori_loop(1, groups, aim_finish, 0)
    arrivals()
    collect(0)
    field_ref[1] = land(0)
    for copy in rim_copies(1):
        copy.start()
    diffuse(1)
    for copy in rim_copies(1):
        copy.wait()
    middle(1)
    chemistry()
    exchange(1)
    collect(1)
    les_out[...] = land(1)
    out = pltpu.make_async_copy(y_ref, lines_out, out_sem)
    out.start()
    out.wait()


def body(
    les,
    lines,
    triplet_start,
    splice_owner,
    splice_line,
    splice_from,
    splice_to,
    chem_counts,
    diffusivity,
    rates,
    frozen_inverse,
):
    groups = lax.axis_size("grid") * lax.axis_size("line")
    _, _, count, species, points = lines.shape
    segments = points // SEG
    slots = min(segments, max(2, 2 * count // groups))
    total = groups * slots
    blocks = total // points
    rows = STEPS * (2 * blocks + 1)

    joint = jnp.dot(frozen_inverse, rates, precision=lax.Precision.HIGHEST)
    twice = jnp.kron(jnp.eye(2, dtype=f32), joint)
    top = lax.reduce_precision(twice, 8, 7)
    rest = lax.reduce_precision(twice - top, 8, 7)
    matrix = jnp.concatenate([top, rest, top], axis=1).astype(bf16)

    dma = pltpu.SemaphoreType.DMA
    field, state = pl.pallas_call(
        functools.partial(kernel, slots),
        out_shape=(
            jax.ShapeDtypeStruct((species, count), f32),
            jax.ShapeDtypeStruct((count, species, points), f32),
        ),
        in_specs=[VMEM, ANY] + [VMEM] * 6 + [SMEM] * 2,
        out_specs=(VMEM, ANY),
        scratch_shapes=[
            pltpu.VMEM((count, species, points), f32),
            pltpu.VMEM((count, species, points), f32),
            pltpu.VMEM((species, points, points), bf16),
            pltpu.VMEM((species, points, points), bf16),
            pltpu.VMEM((STEPS, groups, species, points), f32),
            pltpu.VMEM((groups, species, points), f32),
            pltpu.VMEM((groups, species, points), f32),
            pltpu.VMEM((total, species, points), f32),
            pltpu.VMEM((STEPS, count, points), f32),
            pltpu.VMEM((STEPS, 4, species, count), f32),
            pltpu.VMEM((STEPS, species, count), f32),
            pltpu.VMEM((species, count), f32),
            pltpu.VMEM((blocks, STEPS, points), i32),
            pltpu.VMEM((groups, STEPS, points), i32),
            pltpu.VMEM((total, points), i32),
            pltpu.VMEM((rows, 1, points), i32),
            pltpu.SMEM((rows, 1, points), i32),
            dma,
            dma((2,)),
            dma((STEPS, 4)),
            dma((STEPS, 4)),
            dma((groups,)),
            dma((groups,)),
            dma((STEPS, groups)),
            dma((STEPS, groups)),
            dma,
        ],
        compiler_params=pltpu.CompilerParams(
            collective_id=0, has_side_effects=True, vmem_limit_bytes=40 * 1024 * 1024
        ),
        name="steps",
    )(
        les.reshape(species, count),
        lines.reshape(count, species, points),
        triplet_start.reshape(STEPS, count),
        splice_owner.reshape(STEPS, count),
        splice_line.reshape(STEPS, count),
        splice_from.reshape(STEPS, count),
        splice_to.reshape(STEPS, count),
        matrix,
        diffusivity,
        chem_counts.reshape(count),
    )
    return (field.reshape(les.shape), state.reshape(lines.shape))


def solution(mesh):
    in_specs = (
        P(None, "grid", "line"),
        P("grid", "line", None, None, None),
        P(None, "grid", "line", None),
        P(None, "grid", "line", None, None),
        P(None, "grid", "line", None),
        P(None, "grid", "line", None),
        P(None, "grid", "line", None),
        P("grid", "line", None),
        P(),
        P(),
        P(),
    )
    out_specs = (P(None, "grid", "line"), P("grid", "line", None, None, None))
    return jax.shard_map(body, mesh=mesh, in_specs=in_specs, out_specs=out_specs, check_vma=False)
```

time: 105 us -> 69.8 us (0.66)
  Pallas kernels: 83.9 us -> 57.7 us
  other arithmetic: 4.84 us -> 0.19 us
  local copies, waits for them, and re-layouts: 13.1 us -> 9.34 us
    pallas_call x10 -> x1, Pallas kernels: 83.9 us -> 57.7 us  [body(): pl.pallas_call(functools.partial(kernel, slots), out_shape=(jax.ShapeDtyp...]
    squeeze x8 -> x0, local copies, waits for them, and re-layouts: 1.7 us -> none  [the longest x2 1.46 us: neighbours(): after = lax.slice_in_dim(got[2 * dim - 1], 0, 1, axis=dim)]
    unnamed x36 -> x22, local copies, waits for them, and re-layouts: 8.77 us -> 9.25 us
where the time goes in v1:
time: 69.8 us; the launch traced here: 68.8 us
  Pallas kernels  57.7 us (83%)
  local copies, waits for them, and re-layouts  9.34 us (13%)
  matrix products  0.84 us (1%)
    pallas_call x1, Pallas kernels, body(): pl.pallas_call(functools.partial(kernel, slots), out_shape=(jax.ShapeDtyp...  57.7 us
    unnamed x22, local copies, waits for them, and re-layouts  9.25 us

profile of v1, /device:TPU:0, one launch (start us, length us, event | category | flops | bytes accessed | tf_op | source)
XLA Modules:
  0.0 68.8 jit_solution(4486232829056708686)
XLA Ops:
  0.6 0.0 copy-start
  0.7 0.7 copy-done
  1.3 0.8 %fusion.2 = f32[24,24]{1,0:T(8,128)S(1)} fusion(f32[24,24]{1,0:T(8,128)S(1)} %copy-done, f32[24,24]{1,0:T(8,128)} %param.20), kind=kOutput, calls=%fused_computation.7 | convolution fusion | flops 165888 | bytes 6912 | tf_op jit(solution)/shard_map/dot_general | solution.py:452
  2.2 0.1 broadcast_multiply_fusion
  2.3 0.1 mul.27
  2.4 0.1 pad_maximum_fusion.matrix_ref
  2.5 0.0 copy-start.1
  2.5 1.4 %copy-done.1 = f32[1,1,128,24,128]{4,3,2,1,0:T(8,128)S(1)} copy-done((f32[1,1,128,24,128]{4,3,2,1,0:T(8,128)S(1)}, f32[1,1,128,24,128]{4,3,2,1,0:T(8,128)}, u32[]{:S(2)}) %copy-start.1) | copy-done | bytes 1572888
  3.9 0.0 copy-start.2
  3.9 0.7 %copy-done.2 = f32[24,1,128]{2,1,0:T(1,128)S(1)} copy-done((f32[24,1,128]{2,1,0:T(1,128)S(1)}, f32[24,1,128]{2,1,0:T(1,128)}, u32[]{:S(2)}) %copy-start.2) | copy-done | bytes 12312
  4.6 0.0 copy-start.3
  4.6 0.7 copy-done.3
  5.3 0.0 copy-start.4
  5.3 0.7 copy-done.4
  6.0 0.0 copy-start.5
  6.0 0.7 copy-done.5
  6.6 0.0 copy-start.6
  6.6 0.7 copy-done.6
  7.3 0.7 copy-done.7
  8.0 0.7 copy-done.8
  8.7 0.7 copy-done.9
  9.3 57.7 %steps.1 = (f32[24,128]{1,0:T(8,128)S(1)}, f32[128,24,128]{2,1,0:T(8,128)S(1)}) custom-call(f32[24,128]{1,0:T(8,128)S(1)} %bitcast.16, f32[128,24,128]{2,1,0:T(8,128)S(1)} %bitcast.14, s32[2,128]{1,0:T(2,128)S(1)} %bitcast.18, s32[2,128]{1,0:T(2,128)S(1)} %bitcast.19, s32[2,128]{1,0:T(2,128)S(1)} %bitcast.20, s32[2,128]{1,0:T(2,128)S(1)} %bitcast.21, ...), custom_call_target="tpu_custom_call" | custom-call | tf_op jit(solution)/shard_map/steps/pallas_call | solution.py:459
  67.1 0.6 copy.16
  67.7 1.1 %copy.17 = f32[1,1,128,24,128]{4,3,2,1,0:T(8,128)} copy(f32[1,1,128,24,128]{4,3,2,1,0:T(8,128)S(1)} %bitcast.15) | data formatting | bytes 3145728
  (5 shorter events, 0.0 us)
Async XLA Ops:
  0.6 0.7 %copy-start = (f32[24,24]{1,0:T(8,128)S(1)}, f32[24,24]{1,0:T(8,128)}, u32[]{:S(2)}) copy-start(f32[24,24]{1,0:T(8,128)} %param.21) | copy-start | bytes 6916
  2.5 1.4 %copy-start.1 = (f32[1,1,128,24,128]{4,3,2,1,0:T(8,128)S(1)}, f32[1,1,128,24,128]{4,3,2,1,0:T(8,128)}, u32[]{:S(2)}) copy-start(f32[1,1,128,24,128]{4,3,2,1,0:T(8,128)} %param.12) | copy-start | bytes 4718596
  3.9 0.7 %copy-start.2 = (f32[24,1,128]{2,1,0:T(1,128)S(1)}, f32[24,1,128]{2,1,0:T(1,128)}, u32[]{:S(2)}) copy-start(f32[24,1,128]{2,1,0:T(1,128)} %param.11) | copy-start | bytes 36868
  4.6 0.7 copy-start.3
  5.3 0.7 copy-start.4
  6.0 0.7 copy-start.5
  6.6 0.7 copy-start.6
  7.3 0.7 copy-start.7
  8.0 0.7 copy-start.8
  8.7 0.7 copy-start.9

commit v2 on v1

--- a/solution.py
+++ b/solution.py
@@ -20,7 +20,7 @@
 MESH = pl.DeviceIdType.MESH
 VMEM = pl.BlockSpec(memory_space=pltpu.VMEM)
 SMEM = pl.BlockSpec(memory_space=pltpu.SMEM)
-ANY = pl.BlockSpec(memory_space=pl.ANY)
+HBM = pl.BlockSpec(memory_space=pltpu.HBM)
 f32 = jnp.float32
 bf16 = jnp.bfloat16
 i32 = jnp.int32
@@ -57,8 +57,19 @@
 
 def kernel(
     slots,
+    les_hbm,
+    lines_hbm,
+    start_hbm,
+    owner_hbm,
+    line_hbm,
+    from_hbm,
+    to_hbm,
+    matrix_hbm,
+    coeff_hbm,
+    counts_hbm,
+    les_out,
+    lines_out,
     les_ref,
-    lines_ref,
     start_ref,
     owner_ref,
     line_ref,
@@ -67,8 +78,6 @@
     matrix_ref,
     coeff_ref,
     counts_ref,
-    les_out,
-    lines_out,
     y_ref,
     z_ref,
     m_top,
@@ -96,7 +105,8 @@
     recv_sem,
     out_sem,
 ):
-    species, lines = les_ref.shape
+    parts = out_sem.shape[0] - 1
+    species, _, lines = les_ref.shape
     points = y_ref.shape[2]
     segments = points // SEG
     size = [lax.axis_size(n) for n in NAMES]
@@ -118,7 +128,25 @@
         return carry
 
     lax.fori_loop(1, groups, greet, 0)
-    load = pltpu.make_async_copy(lines_ref, y_ref, load_sem)
+    tables = [
+        pltpu.make_async_copy(source, target, load_sem.at[n])
+        for n, (source, target) in enumerate(
+            [
+                (coeff_hbm, coeff_ref),
+                (owner_hbm, owner_ref),
+                (from_hbm, from_ref),
+                (line_hbm, line_ref),
+                (to_hbm, to_ref),
+                (les_hbm, les_ref),
+                (start_hbm, start_ref),
+                (counts_hbm, counts_ref),
+                (matrix_hbm, matrix_ref),
+            ]
+        )
+    ]
+    load = pltpu.make_async_copy(lines_hbm, y_ref, load_sem.at[len(tables)])
+    for copy in tables:
+        copy.start()
     load.start()
 
     rims = []
@@ -163,7 +191,9 @@
             device_id_type=MESH,
         )
 
-    field_ref[0] = les_ref[...]
+    for copy in tables:
+        copy.wait()
+    field_ref[0] = les_ref[...].reshape(species, lines)
 
     lane = iota((points, points), 1)
     row = iota((points, points), 0)
@@ -368,7 +398,7 @@
 
         lax.fori_loop(1, groups, finish, 0)
 
-    def land(step):
+    def land(step, out):
         base = send_rows + step * (blocks + 1)
 
         def run(n, acc):
@@ -393,7 +423,11 @@
             y_ref[l] = value
             return jnp.where(lane_s == l, jnp.sum(value, axis=1, keepdims=True), sums)
 
-        sums = lax.fori_loop(0, lines, settle, jnp.zeros((species, points), f32), unroll=8)
+        sums = jnp.zeros((species, points), f32)
+        for p in range(parts):
+            sums = lax.fori_loop(p * lines // parts, (p + 1) * lines // parts, settle, sums, unroll=8)
+            if out:
+                out[p].start()
         return 0.5 * mid_ref[...] + (0.5 / points) * sums
 
     load.wait()
@@ -412,7 +446,7 @@
     lax.fori_loop(1, groups, aim_finish, 0)
     arrivals()
     collect(0)
-    field_ref[1] = land(0)
+    field_ref[1] = land(0, None)
     for copy in rim_copies(1):
         copy.start()
     diffuse(1)
@@ -422,10 +456,19 @@
     chemistry()
     exchange(1)
     collect(1)
-    les_out[...] = land(1)
-    out = pltpu.make_async_copy(y_ref, lines_out, out_sem)
-    out.start()
-    out.wait()
+    out = [
+        pltpu.make_async_copy(
+            y_ref.at[pl.ds(p * lines // parts, lines // parts)],
+            lines_out.at[pl.ds(p * lines // parts, lines // parts)],
+            out_sem.at[p],
+        )
+        for p in range(parts)
+    ]
+    les_ref[...] = land(1, out).reshape(species, 1, lines)
+    last = pltpu.make_async_copy(les_ref, les_out, out_sem.at[parts])
+    last.start()
+    for copy in out + [last]:
+        copy.wait()
 
 
 def body(
@@ -459,12 +502,17 @@
     field, state = pl.pallas_call(
         functools.partial(kernel, slots),
         out_shape=(
-            jax.ShapeDtypeStruct((species, count), f32),
+            jax.ShapeDtypeStruct((species, 1, count), f32),
             jax.ShapeDtypeStruct((count, species, points), f32),
         ),
-        in_specs=[VMEM, ANY] + [VMEM] * 6 + [SMEM] * 2,
-        out_specs=(VMEM, ANY),
+        in_specs=[HBM] * 10,
+        out_specs=(HBM, HBM),
         scratch_shapes=[
+            pltpu.VMEM((species, 1, count), f32),
+            *[pltpu.VMEM((STEPS, count), i32)] * 5,
+            pltpu.VMEM(matrix.shape, bf16),
+            pltpu.SMEM((species,), f32),
+            pltpu.SMEM((count,), i32),
             pltpu.VMEM((count, species, points), f32),
             pltpu.VMEM((count, species, points), f32),
             pltpu.VMEM((species, points, points), bf16),
@@ -482,7 +530,7 @@
             pltpu.VMEM((total, points), i32),
             pltpu.VMEM((rows, 1, points), i32),
             pltpu.SMEM((rows, 1, points), i32),
-            dma,
+            dma((10,)),
             dma((2,)),
             dma((STEPS, 4)),
             dma((STEPS, 4)),
@@ -490,14 +538,14 @@
             dma((groups,)),
             dma((STEPS, groups)),
             dma((STEPS, groups)),
-            dma,
+            dma((5,)),
         ],
         compiler_params=pltpu.CompilerParams(
-            collective_id=0, has_side_effects=True, vmem_limit_bytes=40 * 1024 * 1024
+            collective_id=0, has_side_effects=True, vmem_limit_bytes=67043328
         ),
         name="steps",
     )(
-        les.reshape(species, count),
+        les.reshape(species, 1, count),
         lines.reshape(count, species, points),
         triplet_start.reshape(STEPS, count),
         splice_owner.reshape(STEPS, count),

time: 69.8 us -> 65.3 us (0.936)
  local copies, waits for them, and re-layouts: 9.34 us -> 4.05 us
    unnamed x22 -> x2, local copies, waits for them, and re-layouts: 9.25 us -> 3.96 us
where the time goes in v2:
time: 65.3 us; the launch traced here: 64.1 us
  Pallas kernels  57.7 us (88%)
  local copies, waits for them, and re-layouts  4.05 us (6%)
  matrix products  0.86 us (1%)
  other arithmetic  0.8 us (1%)
  between operations  0.66 us (1%)
    pallas_call x1, Pallas kernels, body(): pl.pallas_call(functools.partial(kernel, slots), out_shape=(jax.ShapeDtyp...  57.7 us
    unnamed x2, local copies, waits for them, and re-layouts  3.96 us

profile of v2, /device:TPU:0, one launch (start us, length us, event | category | flops | bytes accessed | tf_op | source)
XLA Modules:
  0.0 64.1 jit_solution(10589535581584947800)
XLA Ops:
  0.6 0.9 %fusion.2 = f32[24,24]{1,0:T(8,128)S(1)} fusion(f32[24,24]{1,0:T(8,128)} %param.21, f32[24,24]{1,0:T(8,128)} %param.20), kind=kOutput, calls=%fused_computation.7 | convolution fusion | flops 165888 | bytes 6912 | tf_op jit(solution)/shard_map/dot_general | solution.py:495
  1.5 0.1 broadcast_multiply_fusion
  1.6 0.1 mul.27
  1.7 0.7 %pad_maximum_fusion.matrix_hbm = bf16[48,144]{1,0:T(8,128)(2,1)} fusion(bf16[48,48]{1,0:T(8,128)(2,1)S(1)} %get-tuple-element.7, bf16[48,48]{1,0:T(8,128)(2,1)S(1)} %get-tuple-element.6), kind=kLoop, calls=%fused_computation.4 | loop fusion | flops 41472 | bytes 23040 | tf_op jit(solution)/shard_map/concatenate | solution.py:499
  2.4 57.7 %steps.1 = (f32[24,1,128]{2,1,0:T(1,128)}, f32[128,24,128]{2,1,0:T(8,128)}) custom-call(f32[24,1,128]{2,1,0:T(1,128)} %les_hbm.1, f32[128,24,128]{2,1,0:T(8,128)} %bitcast.10, s32[2,128]{1,0:T(2,128)} %bitcast.12, s32[2,128]{1,0:T(2,128)} %bitcast.13, s32[2,128]{1,0:T(2,128)} %bitcast.14, s32[2,128]{1,0:T(2,128)} %bitcast.15, s32[2,128]{1,0:T(2,128)} %bitcast.16, ...), custom_call_target="tpu_custom_call" | custom-call | tf_op jit(solution)/shard_map/steps/pallas_call | solution.py:502
  60.1 1.3 %copy.15 = f32[24,1,128]{2,1,0:T(1,128)} copy(f32[24,1,128]{2,1,0:T(1,128)} %get-tuple-element.10) | data formatting | bytes 24576
  61.5 2.7 %copy.16 = f32[1,1,128,24,128]{4,3,2,1,0:T(8,128)} copy(f32[1,1,128,24,128]{4,3,2,1,0:T(8,128)} %bitcast.11) | data formatting | bytes 3145728
  (2 shorter events, 0.0 us)

commit v3 on v2

--- a/solution.py
+++ b/solution.py
@@ -64,7 +64,8 @@
     line_hbm,
     from_hbm,
     to_hbm,
-    matrix_hbm,
+    rates_hbm,
+    frozen_hbm,
     coeff_hbm,
     counts_hbm,
     les_out,
@@ -75,7 +76,8 @@
     line_ref,
     from_ref,
     to_ref,
-    matrix_ref,
+    rates_ref,
+    frozen_ref,
     coeff_ref,
     counts_ref,
     y_ref,
@@ -86,6 +88,10 @@
     recv_0,
     recv_1,
     sums_ref,
+    mask_ref,
+    keep_ref,
+    into_ref,
+    fold_ref,
     weight_ref,
     rim_ref,
     field_ref,
@@ -118,8 +124,8 @@
     recv_refs = (recv_0, recv_1)
 
     def place(j):
-        peer = lax.rem(me + j, groups)
-        return peer, (peer // size[1], lax.rem(peer, size[1]))
+        peer = (me + j) & (groups - 1)
+        return peer, (peer >> bits(size[1]), peer & (size[1] - 1))
 
     barrier = pltpu.get_barrier_semaphore()
 
@@ -140,7 +146,8 @@
                 (les_hbm, les_ref),
                 (start_hbm, start_ref),
                 (counts_hbm, counts_ref),
-                (matrix_hbm, matrix_ref),
+                (rates_hbm, rates_ref),
+                (frozen_hbm, frozen_ref),
             ]
         )
     ]
@@ -172,7 +179,7 @@
     def aim_copy(j):
         peer, device = place(j)
         return pltpu.make_async_remote_copy(
-            src_ref=aim_ref.at[(peer * slots) // points],
+            src_ref=aim_ref.at[(peer * slots) >> bits(points)],
             dst_ref=got_ref.at[me],
             send_sem=aim_send.at[j],
             recv_sem=aim_recv.at[j],
@@ -201,7 +208,8 @@
         owner = owner_ref[step : step + 1, :]
         rank = total_of(when((column(owner) == owner) & (row < lane), 1), 0)
         spot = column(owner * slots + rank)
-        code = column(iota((1, points), 1) * segments + from_ref[step : step + 1, :])
+        turn = (SEG * (rank - from_ref[step : step + 1, :])) & (points - 1)
+        code = column(iota((1, points), 1) * points + turn)
         aim = column(line_ref[step : step + 1, :] * segments + to_ref[step : step + 1, :] + 1)
         for b in range(blocks):
             hit = spot == lane + b * points
@@ -238,7 +246,7 @@
         return carry
 
     lax.fori_loop(1, groups, aim_start, 0)
-    got_ref[me] = aim_ref[(me * slots) // points]
+    got_ref[me] = aim_ref[(me * slots) >> bits(points)]
 
     flat_y = y_ref.reshape(lines * species, points)
     flat_z = z_ref.reshape(lines * species, points)
@@ -261,7 +269,7 @@
             flat_z[pl.ds(s, lines, stride=species), :] = out
             return carry
 
-        lax.fori_loop(0, species, one, 0, unroll=4)
+        lax.fori_loop(0, species, one, 0, unroll=12)
 
     lane_s = lax.broadcasted_iota(i32, (species, points), 1)
 
@@ -275,41 +283,44 @@
         after = pltpu.roll(jnp.where(lane_s == 0, right, field), points - 1, 1)
         mid_ref[...] = field + les_rate * (up + down + before + after - 4.0 * field)
 
-    matrix = matrix_ref[...]
-    chunk = 64
+    joint = jnp.dot(
+        frozen_ref[...], rates_ref[...], precision=lax.Precision.HIGHEST, preferred_element_type=f32
+    )
+    joint_top, joint_rest = halves(joint)
+    wide = (2 * species, 6 * species)
+    place_c = iota(wide, 1)
+    block_c = sum((place_c >= species * n).astype(i32) for n in range(1, 6))
+    pick = jnp.where(
+        iota((species, 6 * species), 0) == (place_c - species * block_c)[:species], 1.0, 0.0
+    ).astype(bf16)
+    twice_top = dot(jnp.concatenate([joint_top.astype(f32)] * 2, axis=0).astype(bf16), pick)
+    twice_rest = dot(jnp.concatenate([joint_rest.astype(f32)] * 2, axis=0).astype(bf16), pick)
+    entries = jnp.where((block_c >> 1) == 1, twice_rest, twice_top)
+    matrix = jnp.where((iota(wide, 0) >= species).astype(i32) == (block_c & 1), entries, 0.0).astype(bf16)
 
     def substep(sub, in_ref, out_ref, lift):
-        def part(c, inner):
-            base = c * chunk
-            mid = mid_ref[...] if lift else None
-            for q in range(0, chunk, 4):
-                columns = []
-                state = []
-                for h in (0, 2):
-                    y = in_ref[pl.ds(base + q + h, 2)].reshape(2 * species, points)
-                    if lift:
-                        add = [
-                            jnp.take_along_axis(
-                                mid, jnp.full((species, points), base + q + h + k, i32), axis=1, mode="promise_in_bounds"
-                            )
-                            for k in (0, 1)
-                        ]
-                        y = y + relax_rate * jnp.concatenate(add, axis=0)
-                    state.append(y)
-                    top, rest = halves(jnp.tanh(y))
-                    columns.append(jnp.concatenate([top, top, rest], axis=0))
-                right = jnp.concatenate(columns, axis=1)
-                change = dot(matrix, right)
-                for h in (0, 1):
-                    for k in (0, 1):
-                        l = base + q + 2 * h + k
-                        factor = jnp.where(counts_ref[l] > sub, f32(1.0), f32(0.0))
-                        rows = slice(k * species, (k + 1) * species)
-                        value = state[h][rows] + factor * change[rows, h * points : (h + 1) * points]
-                        out_ref[l] = value
-            return inner
-
-        lax.fori_loop(0, lines // chunk, part, 0)
+        mid = relax_rate * mid_ref[...] if lift else None
+        for q in range(0, lines, 4):
+            columns = []
+            state = []
+            for h in (0, 2):
+                y = in_ref[pl.ds(q + h, 2)].reshape(2 * species, points)
+                if lift:
+                    add = [
+                        jnp.broadcast_to(mid[:, l : l + 1], (species, points)) for l in (q + h, q + h + 1)
+                    ]
+                    y = y + jnp.concatenate(add, axis=0)
+                state.append(y)
+                top, rest = halves(jnp.tanh(y))
+                columns.append(jnp.concatenate([top, top, rest], axis=0))
+            right = jnp.concatenate(columns, axis=1)
+            change = dot(matrix, right)
+            for h in (0, 1):
+                for k in (0, 1):
+                    l = q + 2 * h + k
+                    factor = jnp.where(counts_ref[l] > sub, f32(1.0), f32(0.0))
+                    rows = slice(k * species, (k + 1) * species)
+                    out_ref[l] = state[h][rows] + factor * change[rows, h * points : (h + 1) * points]
 
     def chemistry():
         substep(0, z_ref, y_ref, True)
@@ -326,11 +337,10 @@
 
     def pack(step, peer):
         tile = jnp.zeros((species, points), f32)
+        first = peer * slots
         for k in range(slots):
-            q = peer * slots + k
-            code = tab_smem[step * blocks + q // points, 0, lax.rem(q, points)]
-            value = z_ref[code >> bits(segments)]
-            value = pltpu.roll(value, (SEG * (k - (code & (segments - 1)))) & (points - 1), 1)
+            code = tab_smem[step * blocks + (first >> bits(points)), 0, (first & (points - 1)) + k]
+            value = pltpu.roll(z_ref[code >> bits(points)], code & (points - 1), 1)
             tile = jnp.where(segment == k, value, tile)
         return tile
 
@@ -353,7 +363,7 @@
         number = iota((total, 1), 0)
         lane_t = iota((total, points), 1)
         number_r = iota((1, total), 1)
-        offset = lax.rem(me * slots, points)
+        offset = (me * slots) & (points - 1)
         mine = offset + (iota((total, points), 0) & (slots - 1))
         for step in range(STEPS):
             for r in range(groups):
@@ -374,16 +384,24 @@
             below = key_r < key_c
             position = total_of(when(below, 1), 1)
             same = total_of(when(below & (line_r == line), 1), 1)
-            value = (number * segments + seg) * 2 + when(same == 0, 1)
+            turn = (SEG * (seg - (number & (slots - 1)))) & (points - 1)
+            value = (number >> bits(slots)) * points + turn
+            kind = seg * 2 + when(same == 0, 1)
             base = send_rows + step * (blocks + 1)
             for b in range(blocks):
-                tab_ref[base + b] = total_of(when(position == lane_t + b * points, value), 0)
+                hit = position == lane_t + b * points
+                tab_ref[base + b] = total_of(when(hit, value), 0)
+                kinds = column(total_of(when(hit, kind), 0))
+                at_b = pl.ds(b * points, points)
+                mask_ref[step, at_b, :] = jnp.where((kinds >> 1) == (lane >> bits(SEG)), splice_weight, 0.0)
+                keep_ref[step, at_b, :] = jnp.where((kinds & 1) == 1, 0.0, 1.0)
             upto = total_of(when(line_c <= lane_t, 1), 0)
             many = total_of(when(line_c == lane_t, 1), 0)
-            tab_ref[base + blocks] = jnp.maximum(upto - 1, 0) * 2 + when(many > 0, 1)
+            tab_ref[base + blocks] = jnp.where(many > 0, upto - 1, total)
             lands = jnp.where(line_r == iota((lines, total), 0), 1.0, 0.0).astype(bf16)
             covers = jnp.where(seg == (lane_t >> bits(SEG)), 1.0, 0.0).astype(bf16)
             weight_ref[step] = 1.0 - splice_weight * dot(lands, covers)
+            into_ref[step] = jnp.where(line_c == lane_t, splice_weight, 0.0)
         rows = STEPS * (blocks + 1)
         copy = pltpu.make_async_copy(
             tab_ref.at[pl.ds(send_rows, rows)], tab_smem.at[pl.ds(send_rows, rows)], tab_sem.at[1]
@@ -398,37 +416,56 @@
 
         lax.fori_loop(1, groups, finish, 0)
 
+    def prepare(step):
+        def rows(j, carry):
+            block = jnp.broadcast_to(into_ref[step, pl.ds(j, 1), :], (SEG, lines))
+            fold_ref[pl.ds(pl.multiple_of(j * SEG, SEG), SEG), :] = block.astype(bf16)
+            return carry
+
+        lax.fori_loop(0, total, rows, 0, unroll=8)
+
+        def scale(l, sums):
+            value = z_ref[l] * weight_ref[step, pl.ds(l, 1), :]
+            z_ref[l] = value
+            return jnp.where(lane_s == l, jnp.sum(value, axis=1, keepdims=True), sums)
+
+        return lax.fori_loop(0, lines, scale, jnp.zeros((species, points), f32), unroll=8)
+
+    def filtered(step, sums):
+        depth = slots * SEG
+
+        def add(r, acc):
+            top, rest = halves(recv_refs[step][r][:, :depth])
+            right = fold_ref[pl.ds(pl.multiple_of(r * depth, depth), depth), :]
+            return acc + dot(jnp.concatenate([top.astype(f32), rest.astype(f32)], axis=0).astype(bf16), right)
+
+        acc = lax.fori_loop(0, groups, add, jnp.zeros((2 * species, points), f32), unroll=8)
+        return 0.5 * mid_ref[...] + (0.5 / points) * (sums + (acc[:species] + acc[species:]))
+
     def land(step, out):
         base = send_rows + step * (blocks + 1)
-
-        def run(n, acc):
-            code = tab_smem[base + n // points, 0, lax.rem(n, points)]
-            first = code & 1
-            seg = (code >> 1) & (segments - 1)
-            number = code >> bits(2 * segments)
-            source = number >> bits(slots)
-            k = number & (slots - 1)
-            value = pltpu.roll(recv_refs[step][source], (SEG * (seg - k)) & (points - 1), 1)
-            value = jnp.where(segment == seg, value, 0.0)
-            acc = value + jnp.where(first == 1, f32(0.0), f32(1.0)) * acc
-            sums_ref[n] = acc
-            return acc
-
-        lax.fori_loop(0, total, run, jnp.zeros((species, points), f32), unroll=8)
-
-        def settle(l, sums):
-            code = tab_smem[base + blocks, 0, l]
-            factor = jnp.where((code & 1) == 1, f32(splice_weight), f32(0.0))
-            value = z_ref[l] * weight_ref[step, pl.ds(l, 1), :] + factor * sums_ref[code >> 1]
-            y_ref[l] = value
-            return jnp.where(lane_s == l, jnp.sum(value, axis=1, keepdims=True), sums)
-
-        sums = jnp.zeros((species, points), f32)
+        sums_ref[total] = jnp.zeros((species, points), f32)
+        acc = jnp.zeros((species, points), f32)
+        for b in range(blocks):
+
+            def run(i, acc):
+                code = tab_smem[base + b, 0, i]
+                value = pltpu.roll(recv_refs[step][code >> bits(points)], code & (points - 1), 1)
+                n = b * points + i
+                acc = value * mask_ref[step, pl.ds(n, 1), :] + acc * keep_ref[step, pl.ds(n, 1), :]
+                sums_ref[n] = acc
+                return acc
+
+            acc = lax.fori_loop(0, points, run, acc, unroll=16)
+
+        def settle(l, carry):
+            y_ref[l] = z_ref[l] + sums_ref[tab_smem[base + blocks, 0, l]]
+            return carry
+
         for p in range(parts):
-            sums = lax.fori_loop(p * lines // parts, (p + 1) * lines // parts, settle, sums, unroll=8)
+            lax.fori_loop(p * lines // parts, (p + 1) * lines // parts, settle, 0, unroll=16)
             if out:
                 out[p].start()
-        return 0.5 * mid_ref[...] + (0.5 / points) * sums
 
     load.wait()
     diffuse(0)
@@ -445,17 +482,23 @@
 
     lax.fori_loop(1, groups, aim_finish, 0)
     arrivals()
+    sums = prepare(0)
     collect(0)
-    field_ref[1] = land(0, None)
+    field_ref[1] = filtered(0, sums)
     for copy in rim_copies(1):
         copy.start()
+    land(0, None)
     diffuse(1)
     for copy in rim_copies(1):
         copy.wait()
     middle(1)
     chemistry()
     exchange(1)
+    sums = prepare(1)
     collect(1)
+    les_ref[...] = filtered(1, sums).reshape(species, 1, lines)
+    last = pltpu.make_async_copy(les_ref, les_out, out_sem.at[parts])
+    last.start()
     out = [
         pltpu.make_async_copy(
             y_ref.at[pl.ds(p * lines // parts, lines // parts)],
@@ -464,11 +507,27 @@
         )
         for p in range(parts)
     ]
-    les_ref[...] = land(1, out).reshape(species, 1, lines)
-    last = pltpu.make_async_copy(les_ref, les_out, out_sem.at[parts])
-    last.start()
+    land(1, out)
     for copy in out + [last]:
         copy.wait()
+
+
+def deliver_kernel(les_in, lines_in, les_out, lines_out, les_ref, lines_ref, in_sem, out_sem):
+    parts = in_sem.shape[0] - 1
+    size = lines_ref.shape[0] // parts
+    pairs = [(les_in, les_ref, les_out)]
+    for p in range(parts):
+        at = pl.ds(p * size, size)
+        pairs.append((lines_in.at[at], lines_ref.at[at], lines_out.at[at]))
+    takes = [pltpu.make_async_copy(a, b, in_sem.at[n]) for n, (a, b, c) in enumerate(pairs)]
+    gives = [pltpu.make_async_copy(b, c, out_sem.at[n]) for n, (a, b, c) in enumerate(pairs)]
+    for take in takes:
+        take.start()
+    for take, give in zip(takes, gives):
+        take.wait()
+        give.start()
+    for give in gives:
+        give.wait()
 
 
 def body(
@@ -492,12 +551,6 @@
     blocks = total // points
     rows = STEPS * (2 * blocks + 1)
 
-    joint = jnp.dot(frozen_inverse, rates, precision=lax.Precision.HIGHEST)
-    twice = jnp.kron(jnp.eye(2, dtype=f32), joint)
-    top = lax.reduce_precision(twice, 8, 7)
-    rest = lax.reduce_precision(twice - top, 8, 7)
-    matrix = jnp.concatenate([top, rest, top], axis=1).astype(bf16)
-
     dma = pltpu.SemaphoreType.DMA
     field, state = pl.pallas_call(
         functools.partial(kernel, slots),
@@ -505,12 +558,13 @@
             jax.ShapeDtypeStruct((species, 1, count), f32),
             jax.ShapeDtypeStruct((count, species, points), f32),
         ),
-        in_specs=[HBM] * 10,
+        in_specs=[HBM] * 11,
         out_specs=(HBM, HBM),
         scratch_shapes=[
             pltpu.VMEM((species, 1, count), f32),
             *[pltpu.VMEM((STEPS, count), i32)] * 5,
-            pltpu.VMEM(matrix.shape, bf16),
+            pltpu.VMEM((species, species), f32),
+            pltpu.VMEM((species, species), f32),
             pltpu.SMEM((species,), f32),
             pltpu.SMEM((count,), i32),
             pltpu.VMEM((count, species, points), f32),
@@ -520,7 +574,11 @@
             pltpu.VMEM((STEPS, groups, species, points), f32),
             pltpu.VMEM((groups, species, points), f32),
             pltpu.VMEM((groups, species, points), f32),
-            pltpu.VMEM((total, species, points), f32),
+            pltpu.VMEM((total + 1, species, points), f32),
+            pltpu.VMEM((STEPS, total, points), f32),
+            pltpu.VMEM((STEPS, total, points), f32),
+            pltpu.VMEM((STEPS, total, count), f32),
+            pltpu.VMEM((total * SEG, count), bf16),
             pltpu.VMEM((STEPS, count, points), f32),
             pltpu.VMEM((STEPS, 4, species, count), f32),
             pltpu.VMEM((STEPS, species, count), f32),
@@ -530,7 +588,7 @@
             pltpu.VMEM((total, points), i32),
             pltpu.VMEM((rows, 1, points), i32),
             pltpu.SMEM((rows, 1, points), i32),
-            dma((10,)),
+            dma((11,)),
             dma((2,)),
             dma((STEPS, 4)),
             dma((STEPS, 4)),
@@ -552,10 +610,25 @@
         splice_line.reshape(STEPS, count),
         splice_from.reshape(STEPS, count),
         splice_to.reshape(STEPS, count),
-        matrix,
+        rates,
+        frozen_inverse,
         diffusivity,
         chem_counts.reshape(count),
     )
+    field, state = pl.pallas_call(
+        deliver_kernel,
+        out_shape=(jax.ShapeDtypeStruct(field.shape, f32), jax.ShapeDtypeStruct(state.shape, f32)),
+        in_specs=[HBM] * 2,
+        out_specs=(HBM, HBM),
+        scratch_shapes=[
+            pltpu.VMEM(field.shape, f32),
+            pltpu.VMEM(state.shape, f32),
+            dma((9,)),
+            dma((9,)),
+        ],
+        compiler_params=pltpu.CompilerParams(vmem_limit_bytes=67043328),
+        name="deliver",
+    )(field, state)
     return (field.reshape(les.shape), state.reshape(lines.shape))
 
 

time: 65.3 us -> 50.6 us (0.77); the launches traced: 64.1 us -> 50.2 us
  Pallas kernels: 57.7 us -> 49.5 us
  local copies, waits for them, and re-layouts: 4.05 us -> 0 us
  matrix products: 0.86 us -> 0 us
  other arithmetic: 0.8 us -> 0 us
    pallas_call x1, Pallas kernels: 57.7 us -> 47.2 us  [body(): pl.pallas_call(functools.partial(kernel, slots), out_shape=(jax.ShapeDtyp...]
    unnamed x2 -> x0, local copies, waits for them, and re-layouts: 3.96 us -> none
    pallas_call x0 -> x1, Pallas kernels: none -> 2.32 us  [body(): pl.pallas_call(deliver_kernel, out_shape=(jax.ShapeDtypeStruct(field.shap...]
    dot_general x1 -> x0, matrix products: 0.86 us -> none  [body(): joint = jnp.dot(frozen_inverse, rates, precision=lax.Precision.HIGHEST)]
    concatenate x1 -> x0, other arithmetic: 0.7 us -> none  [body(): matrix = jnp.concatenate([top, rest, top], axis=1).astype(bf16)]
where the time goes in v3:
time: 50.6 us; the launch traced here: 50.2 us
  Pallas kernels  49.5 us (98%)
  between operations  0.64 us (1%)
    pallas_call x1, Pallas kernels, body(): pl.pallas_call(functools.partial(kernel, slots), out_shape=(jax.ShapeDtyp...  47.2 us
    pallas_call x1, Pallas kernels, body(): pl.pallas_call(deliver_kernel, out_shape=(jax.ShapeDtypeStruct(field.shap...  2.32 us

profile of v3, /device:TPU:0, one launch (start us, length us, event | category | flops | bytes accessed | tf_op | source)
XLA Modules:
  0.0 50.2 jit_solution(17919074576987223833)
XLA Ops:
  0.6 47.2 %steps.1 = (f32[24,1,128]{2,1,0:T(1,128)}, f32[128,24,128]{2,1,0:T(8,128)}) custom-call(f32[24,1,128]{2,1,0:T(1,128)} %les_hbm.1, f32[128,24,128]{2,1,0:T(8,128)} %bitcast.8, s32[2,128]{1,0:T(2,128)} %bitcast.9, s32[2,128]{1,0:T(2,128)} %bitcast.10, s32[2,128]{1,0:T(2,128)} %bitcast.11, s32[2,128]{1,0:T(2,128)} %bitcast.12, s32[2,128]{1,0:T(2,128)} %bitcast.13, ...), custom_call_target="tpu_custom_call" | custom-call | tf_op jit(solution)/shard_map/steps/pallas_call | solution.py:555
  47.8 2.3 %deliver.1 = (f32[24,1,128]{2,1,0:T(1,128)}, f32[128,24,128]{2,1,0:T(8,128)}) custom-call(f32[24,1,128]{2,1,0:T(1,128)} %get-tuple-element.6.les_in, f32[128,24,128]{2,1,0:T(8,128)} %get-tuple-element.7.lines_in), custom_call_target="tpu_custom_call" | custom-call | tf_op jit(solution)/shard_map/deliver/pallas_call | solution.py:618

commit v4 on v3

--- a/solution.py
+++ b/solution.py
@@ -80,6 +80,9 @@
     frozen_ref,
     coeff_ref,
     counts_ref,
+    coeffs_ref,
+    apart_ref,
+    ends_ref,
     y_ref,
     z_ref,
     m_top,
@@ -92,6 +95,7 @@
     keep_ref,
     into_ref,
     fold_ref,
+    both_ref,
     weight_ref,
     rim_ref,
     field_ref,
@@ -198,12 +202,37 @@
             device_id_type=MESH,
         )
 
-    for copy in tables:
+    tables[0].wait()
+    lane = iota((points, points), 1)
+    row = iota((points, points), 0)
+    for n in range(species):
+        coeffs_ref[n : n + 1, :] = jnp.full((1, points), coeff_ref[n], f32)
+    coeff = coeffs_ref[...]
+    root = jnp.sqrt(4.0 * coeff + 1.0)
+    theta = -jnp.log(2.0 * coeff / (2.0 * coeff + 1.0 + root))
+    scale = 1.0 / (root * (1.0 - jnp.exp(-2.0 * points * theta)))
+    along = iota((species, points), 1).astype(f32)
+    apart_ref[...] = scale * (jnp.exp(-along * theta) + jnp.exp((along - 2.0 * points) * theta)) - relax_rate / points
+    ends_ref[...] = scale * (jnp.exp(-(along + 1.0) * theta) + jnp.exp((along + 1.0 - 2.0 * points) * theta))
+    apart = jnp.abs(lane - row)
+    ends = jnp.minimum(lane + row, 2 * points - 2 - lane - row)
+
+    def spread(ref, n, index):
+        value = jnp.broadcast_to(ref[pl.ds(n, 1), :], (points, points))
+        return jnp.take_along_axis(value, index, axis=1, mode="promise_in_bounds")
+
+    def inverse(n, carry):
+        top, rest = halves(spread(apart_ref, n, apart) + spread(ends_ref, n, ends))
+        m_top[n] = top
+        m_rest[n] = rest
+        return carry
+
+    lax.fori_loop(0, species, inverse, 0, unroll=4)
+    for copy in tables[1:]:
         copy.wait()
     field_ref[0] = les_ref[...].reshape(species, lines)
 
-    lane = iota((points, points), 1)
-    row = iota((points, points), 0)
+
     for step in range(STEPS):
         owner = owner_ref[step : step + 1, :]
         rank = total_of(when((column(owner) == owner) & (row < lane), 1), 0)
@@ -218,24 +247,6 @@
     send_rows = STEPS * blocks
     send_table = pltpu.make_async_copy(tab_ref.at[pl.ds(0, send_rows)], tab_smem.at[pl.ds(0, send_rows)], tab_sem.at[0])
     send_table.start()
-
-    apart = jnp.abs(lane - row).astype(f32)
-    both = (lane + row).astype(f32)
-
-    def inverse(s, carry):
-        coeff = jnp.full((8, points), coeff_ref[s], f32)
-        root = jnp.sqrt(4.0 * coeff + 1.0)
-        theta = -jnp.log(2.0 * coeff / (2.0 * coeff + 1.0 + root))
-        scale = 1.0 / (root * (1.0 - jnp.exp(-2.0 * points * theta)))
-        theta = theta[:1]
-        value = jnp.exp(-apart * theta) + jnp.exp((apart - 2.0 * points) * theta)
-        value = value + jnp.exp(-(both + 1.0) * theta) + jnp.exp((both + 1.0 - 2.0 * points) * theta)
-        top, rest = halves(value * scale[:1] - relax_rate / points)
-        m_top[s] = top
-        m_rest[s] = rest
-        return carry
-
-    lax.fori_loop(0, species, inverse, 0)
 
     pl.semaphore_wait(barrier, groups - 1)
     for copy in rim_copies(0):
@@ -345,19 +356,24 @@
         return tile
 
     def exchange(step):
-        def begin(j, carry):
-            peer, _ = place(j)
-            send_ref[step, peer] = pack(step, peer)
-
-            @pl.when(j > 1)
-            def _():
-                data_copy(step, j - 1).start()
+        def begin(i, carry):
+            for n in range(pair):
+                peer, _ = place(pair * i + n)
+                send_ref[step, peer] = pack(step, peer)
+            for n in range(pair):
+                before = pair * (i - 1) + n
+
+                @pl.when(before > 0)
+                def _():
+                    data_copy(step, before).start()
 
             return carry
 
-        lax.fori_loop(1, groups, begin, 0)
-        recv_refs[step][me] = pack(step, me)
-        data_copy(step, groups - 1).start()
+        pair = 2
+        lax.fori_loop(0, groups // pair, begin, 0)
+        recv_refs[step][me] = send_ref[step, me]
+        for n in range(groups - pair, groups):
+            data_copy(step, n).start()
 
     def arrivals():
         number = iota((total, 1), 0)
@@ -419,9 +435,12 @@
     def prepare(step):
         def rows(j, carry):
             block = jnp.broadcast_to(into_ref[step, pl.ds(j, 1), :], (SEG, lines))
-            fold_ref[pl.ds(pl.multiple_of(j * SEG, SEG), SEG), :] = block.astype(bf16)
+            first = (j >> bits(slots)) * points + (j & (slots - 1)) * SEG
+            fold_ref[pl.ds(pl.multiple_of(first, SEG), SEG), :] = block.astype(bf16)
             return carry
 
+        if slots < segments:
+            fold_ref[...] = jnp.zeros_like(fold_ref)
         lax.fori_loop(0, total, rows, 0, unroll=8)
 
         def scale(l, sums):
@@ -432,14 +451,11 @@
         return lax.fori_loop(0, lines, scale, jnp.zeros((species, points), f32), unroll=8)
 
     def filtered(step, sums):
-        depth = slots * SEG
-
-        def add(r, acc):
-            top, rest = halves(recv_refs[step][r][:, :depth])
-            right = fold_ref[pl.ds(pl.multiple_of(r * depth, depth), depth), :]
-            return acc + dot(jnp.concatenate([top.astype(f32), rest.astype(f32)], axis=0).astype(bf16), right)
-
-        acc = lax.fori_loop(0, groups, add, jnp.zeros((2 * species, points), f32), unroll=8)
+        for r in range(groups):
+            value = recv_refs[step][r]
+            rest = value - value.astype(bf16).astype(f32)
+            both_ref[:, r * points : (r + 1) * points] = jnp.concatenate([value, rest], axis=0).astype(bf16)
+        acc = dot(both_ref[...], fold_ref[...])
         return 0.5 * mid_ref[...] + (0.5 / points) * (sums + (acc[:species] + acc[species:]))
 
     def land(step, out):
@@ -456,14 +472,14 @@
                 sums_ref[n] = acc
                 return acc
 
-            acc = lax.fori_loop(0, points, run, acc, unroll=16)
+            acc = lax.fori_loop(0, points, run, acc, unroll=32)
 
         def settle(l, carry):
             y_ref[l] = z_ref[l] + sums_ref[tab_smem[base + blocks, 0, l]]
             return carry
 
         for p in range(parts):
-            lax.fori_loop(p * lines // parts, (p + 1) * lines // parts, settle, 0, unroll=16)
+            lax.fori_loop(p * lines // parts, (p + 1) * lines // parts, settle, 0, unroll=32)
             if out:
                 out[p].start()
 
@@ -567,6 +583,7 @@
             pltpu.VMEM((species, species), f32),
             pltpu.SMEM((species,), f32),
             pltpu.SMEM((count,), i32),
+            *[pltpu.VMEM((species, points), f32)] * 3,
             pltpu.VMEM((count, species, points), f32),
             pltpu.VMEM((count, species, points), f32),
             pltpu.VMEM((species, points, points), bf16),
@@ -578,7 +595,8 @@
             pltpu.VMEM((STEPS, total, points), f32),
             pltpu.VMEM((STEPS, total, points), f32),
             pltpu.VMEM((STEPS, total, count), f32),
-            pltpu.VMEM((total * SEG, count), bf16),
+            pltpu.VMEM((groups * points, count), bf16),
+            pltpu.VMEM((2 * species, groups * points), bf16),
             pltpu.VMEM((STEPS, count, points), f32),
             pltpu.VMEM((STEPS, 4, species, count), f32),
             pltpu.VMEM((STEPS, species, count), f32),

time: 50.6 us -> 48.5 us (0.958)
  Pallas kernels: 49.5 us -> 47 us
    pallas_call x1, Pallas kernels: 47.2 us -> 44.7 us  [body(): pl.pallas_call(functools.partial(kernel, slots), out_shape=(jax.ShapeDtyp...]
where the time goes in v4:
time: 48.5 us; the launch traced here: 47.7 us
  Pallas kernels  47 us (97%)
  between operations  0.64 us (1%)
    pallas_call x1, Pallas kernels, body(): pl.pallas_call(functools.partial(kernel, slots), out_shape=(jax.ShapeDtyp...  44.7 us
    pallas_call x1, Pallas kernels, body(): pl.pallas_call(deliver_kernel, out_shape=(jax.ShapeDtypeStruct(field.shap...  2.32 us

profile of v4, /device:TPU:0, one launch (start us, length us, event | category | flops | bytes accessed | tf_op | source)
XLA Modules:
  0.0 47.7 jit_solution(1505947404758603967)
XLA Ops:
  0.6 44.7 %steps.1 = (f32[24,1,128]{2,1,0:T(1,128)}, f32[128,24,128]{2,1,0:T(8,128)}) custom-call(f32[24,1,128]{2,1,0:T(1,128)} %les_hbm.1, f32[128,24,128]{2,1,0:T(8,128)} %bitcast.8, s32[2,128]{1,0:T(2,128)} %bitcast.9, s32[2,128]{1,0:T(2,128)} %bitcast.10, s32[2,128]{1,0:T(2,128)} %bitcast.11, s32[2,128]{1,0:T(2,128)} %bitcast.12, s32[2,128]{1,0:T(2,128)} %bitcast.13, ...), custom_call_target="tpu_custom_call" | custom-call | tf_op jit(solution)/shard_map/steps/pallas_call | solution.py:571
  45.3 2.3 %deliver.1 = (f32[24,1,128]{2,1,0:T(1,128)}, f32[128,24,128]{2,1,0:T(8,128)}) custom-call(f32[24,1,128]{2,1,0:T(1,128)} %get-tuple-element.6.les_in, f32[128,24,128]{2,1,0:T(8,128)} %get-tuple-element.7.lines_in), custom_call_target="tpu_custom_call" | custom-call | tf_op jit(solution)/shard_map/deliver/pallas_call | solution.py:636

commit v5 on v4

--- a/solution.py
+++ b/solution.py
@@ -11,6 +11,8 @@
 TRIP = 48
 STEPS = 2
 SUBSTEPS = 6
+WAVES = 3
+CHUNK = 64
 
 les_rate = 0.2
 relax_rate = 0.5
@@ -79,18 +81,25 @@
     rates_ref,
     frozen_ref,
     coeff_ref,
-    counts_ref,
+    counts_row,
     coeffs_ref,
     apart_ref,
     ends_ref,
     y_ref,
     z_ref,
-    m_top,
-    m_rest,
+    s_ref,
+    order_ref,
+    matrix_ref,
     send_ref,
-    recv_0,
-    recv_1,
-    sums_ref,
+    recv_00,
+    recv_01,
+    recv_02,
+    recv_10,
+    recv_11,
+    recv_12,
+    sums_0,
+    sums_1,
+    sums_2,
     mask_ref,
     keep_ref,
     into_ref,
@@ -100,6 +109,7 @@
     rim_ref,
     field_ref,
     mid_ref,
+    middle_ref,
     aim_ref,
     got_ref,
     flat_ref,
@@ -116,6 +126,7 @@
     out_sem,
 ):
     parts = out_sem.shape[0] - 1
+    waves = WAVES
     species, _, lines = les_ref.shape
     points = y_ref.shape[2]
     segments = points // SEG
@@ -125,12 +136,15 @@
     me = at[0] * size[1] + at[1]
     total = groups * slots
     blocks = total // points
-    recv_refs = (recv_0, recv_1)
+    recv_refs = ((recv_00, recv_01, recv_02), (recv_10, recv_11, recv_12))
+    sums_refs = (sums_0, sums_1, sums_2)
 
     def place(j):
         peer = (me + j) & (groups - 1)
         return peer, (peer >> bits(size[1]), peer & (size[1] - 1))
 
+    half = groups // 2
+    turns = ((half, groups), (0, half // 2), (half // 2, half))
     barrier = pltpu.get_barrier_semaphore()
 
     def greet(j, carry):
@@ -149,7 +163,7 @@
                 (to_hbm, to_ref),
                 (les_hbm, les_ref),
                 (start_hbm, start_ref),
-                (counts_hbm, counts_ref),
+                (counts_hbm, counts_row),
                 (rates_hbm, rates_ref),
                 (frozen_hbm, frozen_ref),
             ]
@@ -191,11 +205,16 @@
             device_id_type=MESH,
         )
 
-    def data_copy(step, j):
-        peer, device = place(j)
+    def turn_of(i, sign):
+        low = (me + sign * i) & (half - 1)
+        return jnp.where(i < half, me ^ half, me) & half | low
+
+    def data_copy(step, wave, j):
+        peer = turn_of(j, 1)
+        device = (peer >> bits(size[1]), peer & (size[1] - 1))
         return pltpu.make_async_remote_copy(
             src_ref=send_ref.at[step, peer],
-            dst_ref=recv_refs[step].at[me],
+            dst_ref=recv_refs[step][wave].at[j - turns[wave][0]],
             send_sem=send_sem.at[step, j],
             recv_sem=recv_sem.at[step, j],
             device_id=device,
@@ -223,8 +242,7 @@
 
     def inverse(n, carry):
         top, rest = halves(spread(apart_ref, n, apart) + spread(ends_ref, n, ends))
-        m_top[n] = top
-        m_rest[n] = rest
+        matrix_ref[n] = jnp.concatenate([top, rest], axis=1)
         return carry
 
     lax.fori_loop(0, species, inverse, 0, unroll=4)
@@ -237,14 +255,23 @@
         owner = owner_ref[step : step + 1, :]
         rank = total_of(when((column(owner) == owner) & (row < lane), 1), 0)
         spot = column(owner * slots + rank)
+        turn = (owner - me) & (half - 1)
+        key = (jnp.where((owner ^ me) & half == 0, half, 0) + turn) * lines + iota((1, points), 1)
+        spot_sorted = total_of(when(column(key) < key, 1), 0)
+        first = step * (blocks + 2) + blocks
+        tab_ref[first] = spot_sorted
+        sorted_code = column(iota((1, points), 1) * 8 + counts_row[...])
+        order = total_of(when(column(spot_sorted) == lane, sorted_code), 0)
+        tab_ref[first + 1] = order
+        order_ref[step] = jnp.broadcast_to(order >> 3, (species, points))
         turn = (SEG * (rank - from_ref[step : step + 1, :])) & (points - 1)
-        code = column(iota((1, points), 1) * points + turn)
+        code = column(spot_sorted * points + turn)
         aim = column(line_ref[step : step + 1, :] * segments + to_ref[step : step + 1, :] + 1)
         for b in range(blocks):
             hit = spot == lane + b * points
-            tab_ref[step * blocks + b] = total_of(when(hit, code), 0)
+            tab_ref[step * (blocks + 2) + b] = total_of(when(hit, code), 0)
             aim_ref[b, step : step + 1, :] = total_of(when(hit, aim), 0)
-    send_rows = STEPS * blocks
+    send_rows = STEPS * (blocks + 2)
     send_table = pltpu.make_async_copy(tab_ref.at[pl.ds(0, send_rows)], tab_smem.at[pl.ds(0, send_rows)], tab_sem.at[0])
     send_table.start()
 
@@ -275,9 +302,9 @@
         def one(s, carry):
             y = flat_y[pl.ds(s, lines, stride=species), :]
             y = jnp.take_along_axis(y, index, axis=1, mode="promise_in_bounds")
-            top, rest = halves(y)
-            out = dot(top, m_top[s]) + dot(rest, m_top[s]) + dot(top, m_rest[s])
-            flat_z[pl.ds(s, lines, stride=species), :] = out
+            right = matrix_ref[s]
+            out = dot(jnp.concatenate(halves(y), axis=1), jnp.concatenate([right, right], axis=0))
+            flat_z[pl.ds(s, lines, stride=species), :] = out[:, :points] + out[:, points:]
             return carry
 
         lax.fori_loop(0, species, one, 0, unroll=12)
@@ -309,71 +336,80 @@
     entries = jnp.where((block_c >> 1) == 1, twice_rest, twice_top)
     matrix = jnp.where((iota(wide, 0) >= species).astype(i32) == (block_c & 1), entries, 0.0).astype(bf16)
 
-    def substep(sub, in_ref, out_ref, lift):
-        mid = relax_rate * mid_ref[...] if lift else None
-        for q in range(0, lines, 4):
-            columns = []
-            state = []
-            for h in (0, 2):
-                y = in_ref[pl.ds(q + h, 2)].reshape(2 * species, points)
-                if lift:
-                    add = [
-                        jnp.broadcast_to(mid[:, l : l + 1], (species, points)) for l in (q + h, q + h + 1)
-                    ]
-                    y = y + jnp.concatenate(add, axis=0)
-                state.append(y)
-                top, rest = halves(jnp.tanh(y))
-                columns.append(jnp.concatenate([top, top, rest], axis=0))
-            right = jnp.concatenate(columns, axis=1)
-            change = dot(matrix, right)
-            for h in (0, 1):
-                for k in (0, 1):
-                    l = q + 2 * h + k
-                    factor = jnp.where(counts_ref[l] > sub, f32(1.0), f32(0.0))
-                    rows = slice(k * species, (k + 1) * species)
-                    out_ref[l] = state[h][rows] + factor * change[rows, h * points : (h + 1) * points]
-
-    def chemistry():
-        substep(0, z_ref, y_ref, True)
-
-        def two(pair, carry):
-            substep(2 * pair + 1, y_ref, z_ref, False)
-            substep(2 * pair + 2, z_ref, y_ref, False)
-            return carry
-
-        lax.fori_loop(0, SUBSTEPS // 2 - 1, two, 0)
-        substep(SUBSTEPS - 1, y_ref, z_ref, False)
-
     segment = lane_s // SEG
 
     def pack(step, peer):
         tile = jnp.zeros((species, points), f32)
         first = peer * slots
         for k in range(slots):
-            code = tab_smem[step * blocks + (first >> bits(points)), 0, (first & (points - 1)) + k]
-            value = pltpu.roll(z_ref[code >> bits(points)], code & (points - 1), 1)
+            code = tab_smem[step * (blocks + 2) + (first >> bits(points)), 0, (first & (points - 1)) + k]
+            value = pltpu.roll(s_ref[code >> bits(points)], code & (points - 1), 1)
             tile = jnp.where(segment == k, value, tile)
         return tile
 
+    def chemistry(step, base):
+        orders = step * (blocks + 2) + blocks + 1
+        mid = middle_ref[...]
+        codes = [tab_smem[orders, 0, base + i] for i in range(CHUNK)]
+        for sub in range(SUBSTEPS):
+            for q in range(0, CHUNK, 4):
+                columns = []
+                state = []
+                for h in (0, 2):
+                    if sub == 0:
+                        y = jnp.concatenate(
+                            [
+                                z_ref[codes[i] >> 3] + jnp.broadcast_to(mid[:, base + i : base + i + 1], (species, points))
+                                for i in (q + h, q + h + 1)
+                            ],
+                            axis=0,
+                        )
+                    else:
+                        y = s_ref[pl.ds(base + q + h, 2)].reshape(2 * species, points)
+                    state.append(y)
+                    top, rest = halves(jnp.tanh(y))
+                    columns.append(jnp.concatenate([top, top, rest], axis=0))
+                change = dot(matrix, jnp.concatenate(columns, axis=1))
+                for h in (0, 1):
+                    for k in (0, 1):
+                        i = q + 2 * h + k
+                        factor = jnp.where(codes[i] & 7 > sub, f32(1.0), f32(0.0))
+                        rows = slice(k * species, (k + 1) * species)
+                        s_ref[base + i] = state[h][rows] + factor * change[rows, h * points : (h + 1) * points]
+
     def exchange(step):
-        def begin(i, carry):
-            for n in range(pair):
-                peer, _ = place(pair * i + n)
-                send_ref[step, peer] = pack(step, peer)
-            for n in range(pair):
-                before = pair * (i - 1) + n
-
-                @pl.when(before > 0)
+        middle_ref[...] = relax_rate * jnp.take_along_axis(
+            mid_ref[...], order_ref[step], axis=1, mode="promise_in_bounds"
+        )
+        many = CHUNK // slots
+
+        def wrap(i):
+            peer = turn_of(i, 1)
+            send_ref[step, peer] = pack(step, peer)
+
+        for c in range(lines // CHUNK):
+            chemistry(step, c * CHUNK)
+            for n in range(many):
+                wrap(c * many + n)
+            for n in range(many):
+                data_copy(step, 1 if c * many + n < half // 2 else 2, c * many + n).start()
+
+        def near(i, carry):
+            for n in range(2):
+                wrap(half + 2 * i + n)
+            for n in range(2):
+                before = half + 2 * (i - 1) + n
+
+                @pl.when(before > half)
                 def _():
-                    data_copy(step, before).start()
+                    data_copy(step, 0, before).start()
 
             return carry
 
-        pair = 2
-        lax.fori_loop(0, groups // pair, begin, 0)
-        recv_refs[step][me] = send_ref[step, me]
-        for n in range(groups - pair, groups):
-            data_copy(step, n).start()
+        lax.fori_loop(0, half // 2, near, 0)
+        recv_refs[step][0][0] = send_ref[step, me]
+        for n in range(groups - 2, groups):
+            data_copy(step, 0, n).start()
 
     def arrivals():
         number = iota((total, 1), 0)
@@ -391,6 +427,11 @@
             code = code - 1
             line = jnp.where(valid, code >> bits(segments), lines)
             seg = code & (segments - 1)
+            source = number >> bits(slots)
+            deep = (me - source) & (half - 1)
+            late = jnp.where((source ^ me) & half == 0, 0, jnp.where(deep >= half // 2, 2, 1))
+            slot = jnp.where(late == 2, deep - half // 2, deep)
+            line = line + late * (lines + 1)
             line_c = jnp.broadcast_to(line, (total, points))
             line_r = jnp.concatenate(
                 [jnp.transpose(line_c[b * points : (b + 1) * points])[:1] for b in range(blocks)], axis=1
@@ -401,9 +442,9 @@
             position = total_of(when(below, 1), 1)
             same = total_of(when(below & (line_r == line), 1), 1)
             turn = (SEG * (seg - (number & (slots - 1)))) & (points - 1)
-            value = (number >> bits(slots)) * points + turn
+            value = slot * points + turn
             kind = seg * 2 + when(same == 0, 1)
-            base = send_rows + step * (blocks + 1)
+            base = send_rows + step * (blocks + waves)
             for b in range(blocks):
                 hit = position == lane_t + b * points
                 tab_ref[base + b] = total_of(when(hit, value), 0)
@@ -411,31 +452,33 @@
                 at_b = pl.ds(b * points, points)
                 mask_ref[step, at_b, :] = jnp.where((kinds >> 1) == (lane >> bits(SEG)), splice_weight, 0.0)
                 keep_ref[step, at_b, :] = jnp.where((kinds & 1) == 1, 0.0, 1.0)
-            upto = total_of(when(line_c <= lane_t, 1), 0)
-            many = total_of(when(line_c == lane_t, 1), 0)
-            tab_ref[base + blocks] = jnp.where(many > 0, upto - 1, total)
-            lands = jnp.where(line_r == iota((lines, total), 0), 1.0, 0.0).astype(bf16)
+            starts = (0, total // 2, total // 2 + total // 4, total)
+            in_c = jnp.zeros((total, points), jnp.bool_)
+            in_r = jnp.zeros((lines, total), jnp.bool_)
+            for w in range(waves):
+                aim_c = lane_t + w * (lines + 1)
+                upto = total_of(when(line_c <= aim_c, 1), 0)
+                many = total_of(when(line_c == aim_c, 1), 0)
+                tab_ref[base + blocks + w] = jnp.where(many > 0, upto - 1 - starts[w], starts[w + 1] - starts[w])
+                in_c = in_c | (line_c == aim_c)
+                in_r = in_r | (line_r == iota((lines, total), 0) + w * (lines + 1))
+            lands = jnp.where(in_r, 1.0, 0.0).astype(bf16)
             covers = jnp.where(seg == (lane_t >> bits(SEG)), 1.0, 0.0).astype(bf16)
             weight_ref[step] = 1.0 - splice_weight * dot(lands, covers)
-            into_ref[step] = jnp.where(line_c == lane_t, splice_weight, 0.0)
-        rows = STEPS * (blocks + 1)
+            into_ref[step] = jnp.where(in_c, splice_weight, 0.0)
+        rows = STEPS * (blocks + waves)
         copy = pltpu.make_async_copy(
             tab_ref.at[pl.ds(send_rows, rows)], tab_smem.at[pl.ds(send_rows, rows)], tab_sem.at[1]
         )
         copy.start()
         copy.wait()
 
-    def collect(step):
-        def finish(j, carry):
-            data_copy(step, j).wait()
-            return carry
-
-        lax.fori_loop(1, groups, finish, 0)
-
     def prepare(step):
         def rows(j, carry):
             block = jnp.broadcast_to(into_ref[step, pl.ds(j, 1), :], (SEG, lines))
-            first = (j >> bits(slots)) * points + (j & (slots - 1)) * SEG
+            source = j >> bits(slots)
+            first = jnp.where(source & half == me & half, half, 0) + ((me - source) & (half - 1))
+            first = first * points + (j & (slots - 1)) * SEG
             fold_ref[pl.ds(pl.multiple_of(first, SEG), SEG), :] = block.astype(bf16)
             return carry
 
@@ -443,43 +486,76 @@
             fold_ref[...] = jnp.zeros_like(fold_ref)
         lax.fori_loop(0, total, rows, 0, unroll=8)
 
+        places = step * (blocks + 2) + blocks
+
         def scale(l, sums):
-            value = z_ref[l] * weight_ref[step, pl.ds(l, 1), :]
-            z_ref[l] = value
+            value = s_ref[tab_smem[places, 0, l]] * weight_ref[step, pl.ds(l, 1), :]
+            y_ref[l] = value
             return jnp.where(lane_s == l, jnp.sum(value, axis=1, keepdims=True), sums)
 
         return lax.fori_loop(0, lines, scale, jnp.zeros((species, points), f32), unroll=8)
 
-    def filtered(step, sums):
-        for r in range(groups):
-            value = recv_refs[step][r]
+    def collect(step, wave):
+        def finish(j, carry):
+            data_copy(step, wave, j).wait()
+            return carry
+
+        low, high = turns[wave]
+        lax.fori_loop(low + (wave == 0), high, finish, 0)
+
+    def filtered(step, wave):
+        low, high = turns[wave]
+        for i in range(low, high):
+            value = recv_refs[step][wave][i - low]
             rest = value - value.astype(bf16).astype(f32)
-            both_ref[:, r * points : (r + 1) * points] = jnp.concatenate([value, rest], axis=0).astype(bf16)
-        acc = dot(both_ref[...], fold_ref[...])
-        return 0.5 * mid_ref[...] + (0.5 / points) * (sums + (acc[:species] + acc[species:]))
-
-    def land(step, out):
-        base = send_rows + step * (blocks + 1)
-        sums_ref[total] = jnp.zeros((species, points), f32)
-        acc = jnp.zeros((species, points), f32)
-        for b in range(blocks):
-
-            def run(i, acc):
-                code = tab_smem[base + b, 0, i]
-                value = pltpu.roll(recv_refs[step][code >> bits(points)], code & (points - 1), 1)
-                n = b * points + i
-                acc = value * mask_ref[step, pl.ds(n, 1), :] + acc * keep_ref[step, pl.ds(n, 1), :]
-                sums_ref[n] = acc
-                return acc
-
-            acc = lax.fori_loop(0, points, run, acc, unroll=32)
-
-        def settle(l, carry):
-            y_ref[l] = z_ref[l] + sums_ref[tab_smem[base + blocks, 0, l]]
-            return carry
-
+            both_ref[:, i * points : (i + 1) * points] = jnp.concatenate([value, rest], axis=0).astype(bf16)
+        acc = dot(both_ref[:, low * points : high * points], fold_ref[low * points : high * points, :])
+        return acc[:species] + acc[species:]
+
+    def run(step, wave, acc):
+        base = send_rows + step * (blocks + waves)
+        begin = sum(high - low for low, high in turns[:wave]) * slots
+        end = begin + (turns[wave][1] - turns[wave][0]) * slots
+
+        at_row = base + (begin >> bits(points))
+        at_lane = begin & (points - 1)
+        assert at_lane + end - begin <= points
+
+        def one(i, acc):
+            code = tab_smem[at_row, 0, at_lane + i]
+            value = pltpu.roll(recv_refs[step][wave][code >> bits(points)], code & (points - 1), 1)
+            acc = value * mask_ref[step, pl.ds(begin + i, 1), :] + acc * keep_ref[step, pl.ds(begin + i, 1), :]
+            sums_refs[wave][i] = acc
+            return acc
+
+        sums_refs[wave][end - begin] = jnp.zeros((species, points), f32)
+        lax.fori_loop(0, end - begin, one, jnp.zeros((species, points), f32), unroll=32)
+
+    def receive(step, sums, les_done, out):
+        base = send_rows + step * (blocks + waves)
+
+        def settle(which):
+            def one(l, carry):
+                value = y_ref[l]
+                for w in which:
+                    value = value + sums_refs[w][tab_smem[base + blocks + w, 0, l]]
+                y_ref[l] = value
+                return carry
+
+            return one
+
+        for wave in range(waves):
+            collect(step, wave)
+            sums = sums + filtered(step, wave)
+            if wave + 1 < waves:
+                run(step, wave, None)
+            if wave + 2 == waves:
+                lax.fori_loop(0, lines, settle(range(waves - 1)), 0, unroll=8)
+        les_done(0.5 * mid_ref[...] + (0.5 / points) * sums)
+        run(step, waves - 1, None)
         for p in range(parts):
-            lax.fori_loop(p * lines // parts, (p + 1) * lines // parts, settle, 0, unroll=32)
+            low, high = p * lines // parts, (p + 1) * lines // parts
+            lax.fori_loop(low, high, settle((waves - 1,)), 0, unroll=32)
             if out:
                 out[p].start()
 
@@ -489,7 +565,6 @@
         copy.wait()
     middle(0)
     send_table.wait()
-    chemistry()
     exchange(0)
 
     def aim_finish(j, carry):
@@ -499,22 +574,20 @@
     lax.fori_loop(1, groups, aim_finish, 0)
     arrivals()
     sums = prepare(0)
-    collect(0)
-    field_ref[1] = filtered(0, sums)
-    for copy in rim_copies(1):
-        copy.start()
-    land(0, None)
+
+    def again(field):
+        field_ref[1] = field
+        for copy in rim_copies(1):
+            copy.start()
+
+    receive(0, sums, again, None)
     diffuse(1)
     for copy in rim_copies(1):
         copy.wait()
     middle(1)
-    chemistry()
     exchange(1)
     sums = prepare(1)
-    collect(1)
-    les_ref[...] = filtered(1, sums).reshape(species, 1, lines)
     last = pltpu.make_async_copy(les_ref, les_out, out_sem.at[parts])
-    last.start()
     out = [
         pltpu.make_async_copy(
             y_ref.at[pl.ds(p * lines // parts, lines // parts)],
@@ -523,7 +596,12 @@
         )
         for p in range(parts)
     ]
-    land(1, out)
+
+    def finish(field):
+        les_ref[...] = field.reshape(species, 1, lines)
+        last.start()
+
+    receive(1, sums, finish, out)
     for copy in out + [last]:
         copy.wait()
 
@@ -565,7 +643,7 @@
     slots = min(segments, max(2, 2 * count // groups))
     total = groups * slots
     blocks = total // points
-    rows = STEPS * (2 * blocks + 1)
+    rows = STEPS * (2 * blocks + 2 + WAVES)
 
     dma = pltpu.SemaphoreType.DMA
     field, state = pl.pallas_call(
@@ -582,16 +660,20 @@
             pltpu.VMEM((species, species), f32),
             pltpu.VMEM((species, species), f32),
             pltpu.SMEM((species,), f32),
-            pltpu.SMEM((count,), i32),
+            pltpu.VMEM((1, count), i32),
             *[pltpu.VMEM((species, points), f32)] * 3,
             pltpu.VMEM((count, species, points), f32),
             pltpu.VMEM((count, species, points), f32),
-            pltpu.VMEM((species, points, points), bf16),
-            pltpu.VMEM((species, points, points), bf16),
+            pltpu.VMEM((count, species, points), f32),
+            pltpu.VMEM((STEPS, species, count), i32),
+            pltpu.VMEM((species, points, 2 * points), bf16),
             pltpu.VMEM((STEPS, groups, species, points), f32),
-            pltpu.VMEM((groups, species, points), f32),
-            pltpu.VMEM((groups, species, points), f32),
-            pltpu.VMEM((total + 1, species, points), f32),
+            *[
+                pltpu.VMEM((groups // part, species, points), f32)
+                for part in (2, 4, 4) * STEPS
+            ],
+            pltpu.VMEM((total // 2 + 1, species, points), f32),
+            *[pltpu.VMEM((total // 4 + 1, species, points), f32)] * 2,
             pltpu.VMEM((STEPS, total, points), f32),
             pltpu.VMEM((STEPS, total, points), f32),
             pltpu.VMEM((STEPS, total, count), f32),
@@ -600,6 +682,7 @@
             pltpu.VMEM((STEPS, count, points), f32),
             pltpu.VMEM((STEPS, 4, species, count), f32),
             pltpu.VMEM((STEPS, species, count), f32),
+            pltpu.VMEM((species, count), f32),
             pltpu.VMEM((species, count), f32),
             pltpu.VMEM((blocks, STEPS, points), i32),
             pltpu.VMEM((groups, STEPS, points), i32),
@@ -631,7 +714,7 @@
         rates,
         frozen_inverse,
         diffusivity,
-        chem_counts.reshape(count),
+        chem_counts.reshape(1, count),
     )
     field, state = pl.pallas_call(
         deliver_kernel,

time: 48.5 us -> 46.9 us (0.967); the launches traced: 47.7 us -> 46.6 us
  Pallas kernels: 47 us -> 46 us
    pallas_call x1, Pallas kernels: 44.7 us -> 43.7 us  [body(): pl.pallas_call(functools.partial(kernel, slots), out_shape=(jax.ShapeDtyp...]
where the time goes in v5:
time: 46.9 us; the launch traced here: 46.6 us
  Pallas kernels  46 us (98%)
  between operations  0.64 us (1%)
    pallas_call x1, Pallas kernels, body(): pl.pallas_call(functools.partial(kernel, slots), out_shape=(jax.ShapeDtyp...  43.7 us
    pallas_call x1, Pallas kernels, body(): pl.pallas_call(deliver_kernel, out_shape=(jax.ShapeDtypeStruct(field.shap...  2.32 us

profile of v5, /device:TPU:0, one launch (start us, length us, event | category | flops | bytes accessed | tf_op | source)
XLA Modules:
  0.0 46.6 jit_solution(3245366654004607365)
XLA Ops:
  0.6 43.7 %steps.1 = (f32[24,1,128]{2,1,0:T(1,128)}, f32[128,24,128]{2,1,0:T(8,128)}) custom-call(f32[24,1,128]{2,1,0:T(1,128)} %les_hbm.1, f32[128,24,128]{2,1,0:T(8,128)} %bitcast.8, s32[2,128]{1,0:T(2,128)} %bitcast.9, s32[2,128]{1,0:T(2,128)} %bitcast.10, s32[2,128]{1,0:T(2,128)} %bitcast.11, s32[2,128]{1,0:T(2,128)} %bitcast.12, s32[2,128]{1,0:T(2,128)} %bitcast.13, ...), custom_call_target="tpu_custom_call" | custom-call | tf_op jit(solution)/shard_map/steps/pallas_call | solution.py:649
  44.3 2.3 %deliver.1 = (f32[24,1,128]{2,1,0:T(1,128)}, f32[128,24,128]{2,1,0:T(8,128)}) custom-call(f32[24,1,128]{2,1,0:T(1,128)} %get-tuple-element.6.les_in, f32[128,24,128]{2,1,0:T(8,128)} %get-tuple-element.7.lines_in), custom_call_target="tpu_custom_call" | custom-call | tf_op jit(solution)/shard_map/deliver/pallas_call | solution.py:719

commit v6 on v5

--- a/solution.py
+++ b/solution.py
@@ -72,6 +72,10 @@
     counts_hbm,
     les_out,
     lines_out,
+    tiles_out,
+    mask_out,
+    keep_out,
+    table_out,
     les_ref,
     start_ref,
     owner_ref,
@@ -125,7 +129,7 @@
     recv_sem,
     out_sem,
 ):
-    parts = out_sem.shape[0] - 1
+    parts = out_sem.shape[0] - 6
     waves = WAVES
     species, _, lines = les_ref.shape
     points = y_ref.shape[2]
@@ -151,7 +155,6 @@
         pl.semaphore_signal(barrier, inc=1, device_id=place(j)[1], device_id_type=MESH)
         return carry
 
-    lax.fori_loop(1, groups, greet, 0)
     tables = [
         pltpu.make_async_copy(source, target, load_sem.at[n])
         for n, (source, target) in enumerate(
@@ -173,6 +176,7 @@
     for copy in tables:
         copy.start()
     load.start()
+    lax.fori_loop(1, groups, greet, 0)
 
     rims = []
     for axis in (0, 1):
@@ -245,7 +249,7 @@
         matrix_ref[n] = jnp.concatenate([top, rest], axis=1)
         return carry
 
-    lax.fori_loop(0, species, inverse, 0, unroll=4)
+    lax.fori_loop(0, species, inverse, 0, unroll=8)
     for copy in tables[1:]:
         copy.wait()
     field_ref[0] = les_ref[...].reshape(species, lines)
@@ -546,18 +550,20 @@
 
         for wave in range(waves):
             collect(step, wave)
-            sums = sums + filtered(step, wave)
             if wave + 1 < waves:
                 run(step, wave, None)
             if wave + 2 == waves:
                 lax.fori_loop(0, lines, settle(range(waves - 1)), 0, unroll=8)
+                for copy in out[0]:
+                    copy.start()
+            if wave + 1 == waves:
+                for copy in out[1]:
+                    copy.start()
+            sums = sums + filtered(step, wave)
         les_done(0.5 * mid_ref[...] + (0.5 / points) * sums)
-        run(step, waves - 1, None)
-        for p in range(parts):
-            low, high = p * lines // parts, (p + 1) * lines // parts
-            lax.fori_loop(low, high, settle((waves - 1,)), 0, unroll=32)
-            if out:
-                out[p].start()
+        if not out[0]:
+            run(step, waves - 1, None)
+            lax.fori_loop(0, lines, settle((waves - 1,)), 0, unroll=32)
 
     load.wait()
     diffuse(0)
@@ -580,46 +586,91 @@
         for copy in rim_copies(1):
             copy.start()
 
-    receive(0, sums, again, None)
+    receive(0, sums, again, ((), ()))
     diffuse(1)
     for copy in rim_copies(1):
         copy.wait()
     middle(1)
     exchange(1)
     sums = prepare(1)
-    last = pltpu.make_async_copy(les_ref, les_out, out_sem.at[parts])
-    out = [
-        pltpu.make_async_copy(
-            y_ref.at[pl.ds(p * lines // parts, lines // parts)],
-            lines_out.at[pl.ds(p * lines // parts, lines // parts)],
-            out_sem.at[p],
-        )
-        for p in range(parts)
+    final = STEPS - 1
+    begin = total - total // 4
+    base = send_rows + final * (blocks + waves)
+    pairs = [
+        (mask_ref.at[final, pl.ds(begin, total - begin)], mask_out),
+        (keep_ref.at[final, pl.ds(begin, total - begin)], keep_out),
+        (tab_ref.at[base + (begin >> bits(points))], table_out.at[0]),
+        (tab_ref.at[base + blocks + waves - 1], table_out.at[1]),
     ]
+    for p in range(parts):
+        at_p = pl.ds(p * lines // parts, lines // parts)
+        pairs.append((y_ref.at[at_p], lines_out.at[at_p]))
+    early = [pltpu.make_async_copy(a, b, out_sem.at[n]) for n, (a, b) in enumerate(pairs)]
+    last = pltpu.make_async_copy(les_ref, les_out, out_sem.at[parts + 4])
+    tiles = pltpu.make_async_copy(recv_refs[final][waves - 1], tiles_out, out_sem.at[parts + 5])
 
     def finish(field):
         les_ref[...] = field.reshape(species, 1, lines)
         last.start()
 
-    receive(1, sums, finish, out)
-    for copy in out + [last]:
+    receive(1, sums, finish, (early, [tiles]))
+    for copy in early + [tiles, last]:
         copy.wait()
 
 
-def deliver_kernel(les_in, lines_in, les_out, lines_out, les_ref, lines_ref, in_sem, out_sem):
-    parts = in_sem.shape[0] - 1
-    size = lines_ref.shape[0] // parts
-    pairs = [(les_in, les_ref, les_out)]
-    for p in range(parts):
-        at = pl.ds(p * size, size)
-        pairs.append((lines_in.at[at], lines_ref.at[at], lines_out.at[at]))
-    takes = [pltpu.make_async_copy(a, b, in_sem.at[n]) for n, (a, b, c) in enumerate(pairs)]
-    gives = [pltpu.make_async_copy(b, c, out_sem.at[n]) for n, (a, b, c) in enumerate(pairs)]
+def deliver_kernel(
+    les_in,
+    lines_in,
+    tiles_in,
+    mask_in,
+    keep_in,
+    table_in,
+    les_out,
+    lines_out,
+    les_ref,
+    lines_ref,
+    tiles_ref,
+    mask_ref,
+    keep_ref,
+    table_ref,
+    sums_ref,
+    in_sem,
+    out_sem,
+):
+    lines, species, points = lines_ref.shape
+    parts = out_sem.shape[0] - 1
+    size = lines // parts
+    many = mask_ref.shape[0]
+    small = [(table_in, table_ref), (tiles_in, tiles_ref), (mask_in, mask_ref), (keep_in, keep_ref), (les_in, les_ref)]
+    at = [pl.ds(p * size, size) for p in range(parts)]
+    takes = small + [(lines_in.at[a], lines_ref.at[a]) for a in at]
+    takes = [pltpu.make_async_copy(a, b, in_sem.at[n]) for n, (a, b) in enumerate(takes)]
+    gives = [(lines_ref.at[a], lines_out.at[a]) for a in at] + [(les_ref, les_out)]
+    gives = [pltpu.make_async_copy(a, b, out_sem.at[n]) for n, (a, b) in enumerate(gives)]
     for take in takes:
         take.start()
-    for take, give in zip(takes, gives):
+    for take in takes[: len(small)]:
         take.wait()
-        give.start()
+    gives[parts].start()
+
+    def run(i, acc):
+        code = table_ref[0, 0, points - many + i]
+        value = pltpu.roll(tiles_ref[code >> bits(points)], code & (points - 1), 1)
+        acc = value * mask_ref[pl.ds(i, 1), :] + acc * keep_ref[pl.ds(i, 1), :]
+        sums_ref[i] = acc
+        return acc
+
+    sums_ref[many] = jnp.zeros((species, points), f32)
+    lax.fori_loop(0, many, run, jnp.zeros((species, points), f32), unroll=32)
+
+    def settle(l, carry):
+        lines_ref[l] = lines_ref[l] + sums_ref[table_ref[1, 0, l]]
+        return carry
+
+    for p in range(parts):
+        takes[len(small) + p].wait()
+        lax.fori_loop(p * size, (p + 1) * size, settle, 0, unroll=size)
+        gives[p].start()
     for give in gives:
         give.wait()
 
@@ -646,14 +697,19 @@
     rows = STEPS * (2 * blocks + 2 + WAVES)
 
     dma = pltpu.SemaphoreType.DMA
-    field, state = pl.pallas_call(
+    quarter = total // 4
+    field, *rest = pl.pallas_call(
         functools.partial(kernel, slots),
         out_shape=(
             jax.ShapeDtypeStruct((species, 1, count), f32),
             jax.ShapeDtypeStruct((count, species, points), f32),
+            jax.ShapeDtypeStruct((groups // 4, species, points), f32),
+            jax.ShapeDtypeStruct((quarter, points), f32),
+            jax.ShapeDtypeStruct((quarter, points), f32),
+            jax.ShapeDtypeStruct((2, 1, points), i32),
         ),
         in_specs=[HBM] * 11,
-        out_specs=(HBM, HBM),
+        out_specs=(HBM,) * 6,
         scratch_shapes=[
             pltpu.VMEM((species, 1, count), f32),
             *[pltpu.VMEM((STEPS, count), i32)] * 5,
@@ -697,7 +753,7 @@
             dma((groups,)),
             dma((STEPS, groups)),
             dma((STEPS, groups)),
-            dma((5,)),
+            dma((10,)),
         ],
         compiler_params=pltpu.CompilerParams(
             collective_id=0, has_side_effects=True, vmem_limit_bytes=67043328
@@ -718,18 +774,26 @@
     )
     field, state = pl.pallas_call(
         deliver_kernel,
-        out_shape=(jax.ShapeDtypeStruct(field.shape, f32), jax.ShapeDtypeStruct(state.shape, f32)),
-        in_specs=[HBM] * 2,
+        out_shape=(
+            jax.ShapeDtypeStruct(field.shape, f32),
+            jax.ShapeDtypeStruct((count, species, points), f32),
+        ),
+        in_specs=[HBM] * 6,
         out_specs=(HBM, HBM),
         scratch_shapes=[
             pltpu.VMEM(field.shape, f32),
-            pltpu.VMEM(state.shape, f32),
-            dma((9,)),
+            pltpu.VMEM((count, species, points), f32),
+            pltpu.VMEM((groups // 4, species, points), f32),
+            pltpu.VMEM((quarter, points), f32),
+            pltpu.VMEM((quarter, points), f32),
+            pltpu.SMEM((2, 1, points), i32),
+            pltpu.VMEM((quarter + 1, species, points), f32),
+            dma((13,)),
             dma((9,)),
         ],
         compiler_params=pltpu.CompilerParams(vmem_limit_bytes=67043328),
         name="deliver",
-    )(field, state)
+    )(field, *rest)
     return (field.reshape(les.shape), state.reshape(lines.shape))
 
 

time: 46.9 us -> 45.8 us (0.977)
  Pallas kernels: 46 us -> 44.9 us
    pallas_call x1, Pallas kernels: 43.7 us -> 42.3 us  [body(): pl.pallas_call(functools.partial(kernel, slots), out_shape=(jax.ShapeDtyp...]
where the time goes in v6:
time: 45.8 us; the launch traced here: 45.6 us
  Pallas kernels  44.9 us (98%)
  between operations  0.64 us (1%)
    pallas_call x1, Pallas kernels, body(): pl.pallas_call(functools.partial(kernel, slots), out_shape=(jax.ShapeDtyp...  42.3 us
    pallas_call x1, Pallas kernels, body(): pl.pallas_call(deliver_kernel, out_shape=(jax.ShapeDtypeStruct(field.shap...  2.59 us

profile of v6, /device:TPU:0, one launch (start us, length us, event | category | flops | bytes accessed | tf_op | source)
XLA Modules:
  0.0 45.6 jit_solution(10054965229672463787)
XLA Ops:
  0.6 42.3 %steps.1 = (f32[24,1,128]{2,1,0:T(1,128)}, f32[128,24,128]{2,1,0:T(8,128)}, f32[8,24,128]{2,1,0:T(8,128)}, f32[64,128]{1,0:T(8,128)}, f32[64,128]{1,0:T(8,128)}, /*index=5*/s32[2,1,128]{2,1,0:T(1,128)}) custom-call(f32[24,1,128]{2,1,0:T(1,128)} %les_hbm.1, f32[128,24,128]{2,1,0:T(8,128)} %bitcast.8, s32[2,128]{1,0:T(2,128)} %bitcast.9, s32[2,128]{1,0:T(2,128)} %bitcast.10, ...), custom_call_target="tpu_custom_call" | custom-call | tf_op jit(solution)/shard_map/steps/pallas_call | solution.py:701
  43.0 2.6 %deliver.1 = (f32[24,1,128]{2,1,0:T(1,128)}, f32[128,24,128]{2,1,0:T(8,128)}) custom-call(f32[24,1,128]{2,1,0:T(1,128)} %get-tuple-element.10.les_in, f32[128,24,128]{2,1,0:T(8,128)} %get-tuple-element.11.lines_in, f32[8,24,128]{2,1,0:T(8,128)} %get-tuple-element.12.tiles_in, f32[64,128]{1,0:T(8,128)} %get-tuple-element.13.mask_in, ...), custom_call_target="tpu_custom_call" | custom-call | tf_op jit(solution)/shard_map/deliver/pallas_call | solution.py:775

commit v7 on v6

--- a/solution.py
+++ b/solution.py
@@ -176,6 +176,7 @@
     for copy in tables:
         copy.start()
     load.start()
+    rim_ref[...] = jnp.zeros_like(rim_ref)
     lax.fori_loop(1, groups, greet, 0)
 
     rims = []
@@ -197,6 +198,17 @@
             )
             for k in range(4)
         ]
+
+    inner = [at[0] < size[0] - 1, at[0] > 0, at[1] < size[1] - 1, at[1] > 0]
+
+    def rim_start(step):
+        for k, copy in enumerate(rim_copies(step)):
+            pl.when(inner[k])(copy.start)
+
+    def rim_wait(step):
+        for k, copy in enumerate(rim_copies(step)):
+            pl.when(inner[k])(copy.wait_send)
+            pl.when(inner[k ^ 1])(copy.wait_recv)
 
     def aim_copy(j):
         peer, device = place(j)
@@ -253,6 +265,8 @@
     for copy in tables[1:]:
         copy.wait()
     field_ref[0] = les_ref[...].reshape(species, lines)
+    pl.semaphore_wait(barrier, groups - 1)
+    rim_start(0)
 
 
     for step in range(STEPS):
@@ -279,9 +293,6 @@
     send_table = pltpu.make_async_copy(tab_ref.at[pl.ds(0, send_rows)], tab_smem.at[pl.ds(0, send_rows)], tab_sem.at[0])
     send_table.start()
 
-    pl.semaphore_wait(barrier, groups - 1)
-    for copy in rim_copies(0):
-        copy.start()
 
     def aim_start(j, carry):
         aim_copy(j).start()
@@ -317,10 +328,7 @@
 
     def middle(step):
         field = field_ref[step]
-        up = jnp.where(at[0] > 0, rim_ref[step, 0], 0.0)
-        down = jnp.where(at[0] < size[0] - 1, rim_ref[step, 1], 0.0)
-        left = jnp.where(at[1] > 0, rim_ref[step, 2], 0.0)
-        right = jnp.where(at[1] < size[1] - 1, rim_ref[step, 3], 0.0)
+        up, down, left, right = (rim_ref[step, k] for k in range(4))
         before = pltpu.roll(jnp.where(lane_s == points - 1, left, field), 1, 1)
         after = pltpu.roll(jnp.where(lane_s == 0, right, field), points - 1, 1)
         mid_ref[...] = field + les_rate * (up + down + before + after - 4.0 * field)
@@ -567,8 +575,7 @@
 
     load.wait()
     diffuse(0)
-    for copy in rim_copies(0):
-        copy.wait()
+    rim_wait(0)
     middle(0)
     send_table.wait()
     exchange(0)
@@ -583,13 +590,11 @@
 
     def again(field):
         field_ref[1] = field
-        for copy in rim_copies(1):
-            copy.start()
+        rim_start(1)
 
     receive(0, sums, again, ((), ()))
     diffuse(1)
-    for copy in rim_copies(1):
-        copy.wait()
+    rim_wait(1)
     middle(1)
     exchange(1)
     sums = prepare(1)

time: 45.8 us -> 45.2 us (0.987)
  Pallas kernels: 44.9 us -> 44.3 us
    pallas_call x1, Pallas kernels: 42.3 us -> 41.8 us  [body(): pl.pallas_call(functools.partial(kernel, slots), out_shape=(jax.ShapeDtyp...]
where the time goes in v7:
time: 45.2 us; the launch traced here: 45 us
  Pallas kernels  44.3 us (98%)
  between operations  0.64 us (1%)
    pallas_call x1, Pallas kernels, body(): pl.pallas_call(functools.partial(kernel, slots), out_shape=(jax.ShapeDtyp...  41.8 us
    pallas_call x1, Pallas kernels, body(): pl.pallas_call(deliver_kernel, out_shape=(jax.ShapeDtypeStruct(field.shap...  2.59 us

profile of v7, /device:TPU:0, one launch (start us, length us, event | category | flops | bytes accessed | tf_op | source)
XLA Modules:
  0.0 45.0 jit_solution(14933103335572612349)
XLA Ops:
  0.6 41.8 %steps.1 = (f32[24,1,128]{2,1,0:T(1,128)}, f32[128,24,128]{2,1,0:T(8,128)}, f32[8,24,128]{2,1,0:T(8,128)}, f32[64,128]{1,0:T(8,128)}, f32[64,128]{1,0:T(8,128)}, /*index=5*/s32[2,1,128]{2,1,0:T(1,128)}) custom-call(f32[24,1,128]{2,1,0:T(1,128)} %les_hbm.1, f32[128,24,128]{2,1,0:T(8,128)} %bitcast.8, s32[2,128]{1,0:T(2,128)} %bitcast.9, s32[2,128]{1,0:T(2,128)} %bitcast.10, ...), custom_call_target="tpu_custom_call" | custom-call | tf_op jit(solution)/shard_map/steps/pallas_call | solution.py:706
  42.4 2.6 %deliver.1 = (f32[24,1,128]{2,1,0:T(1,128)}, f32[128,24,128]{2,1,0:T(8,128)}) custom-call(f32[24,1,128]{2,1,0:T(1,128)} %get-tuple-element.10.les_in, f32[128,24,128]{2,1,0:T(8,128)} %get-tuple-element.11.lines_in, f32[8,24,128]{2,1,0:T(8,128)} %get-tuple-element.12.tiles_in, f32[64,128]{1,0:T(8,128)} %get-tuple-element.13.mask_in, ...), custom_call_target="tpu_custom_call" | custom-call | tf_op jit(solution)/shard_map/deliver/pallas_call | solution.py:780

commit v8 on v7

--- a/solution.py
+++ b/solution.py
@@ -294,13 +294,6 @@
     send_table.start()
 
 
-    def aim_start(j, carry):
-        aim_copy(j).start()
-        return carry
-
-    lax.fori_loop(1, groups, aim_start, 0)
-    got_ref[me] = aim_ref[(me * slots) >> bits(points)]
-
     flat_y = y_ref.reshape(lines * species, points)
     flat_z = z_ref.reshape(lines * species, points)
 
@@ -401,10 +394,12 @@
 
         for c in range(lines // CHUNK):
             chemistry(step, c * CHUNK)
-            for n in range(many):
-                wrap(c * many + n)
-            for n in range(many):
-                data_copy(step, 1 if c * many + n < half // 2 else 2, c * many + n).start()
+            for n in range(many + 2):
+                if n < many:
+                    wrap(c * many + n)
+                if n >= 2:
+                    turn = c * many + n - 2
+                    data_copy(step, 1 if turn < half // 2 else 2, turn).start()
 
         def near(i, carry):
             for n in range(2):
@@ -575,6 +570,13 @@
 
     load.wait()
     diffuse(0)
+    def aim_start(j, carry):
+        aim_copy(j).start()
+        return carry
+
+    lax.fori_loop(1, groups, aim_start, 0)
+    got_ref[me] = aim_ref[(me * slots) >> bits(points)]
+
     rim_wait(0)
     middle(0)
     send_table.wait()
@@ -793,8 +795,8 @@
             pltpu.VMEM((quarter, points), f32),
             pltpu.SMEM((2, 1, points), i32),
             pltpu.VMEM((quarter + 1, species, points), f32),
-            dma((13,)),
             dma((9,)),
+            dma((5,)),
         ],
         compiler_params=pltpu.CompilerParams(vmem_limit_bytes=67043328),
         name="deliver",

time: 45.2 us -> 45.2 us (level)
  no operation moved by 1% of the time
where the time goes in v8:
time: 45.2 us; the launch traced here: 45 us
  Pallas kernels  44.3 us (98%)
  between operations  0.64 us (1%)
    pallas_call x1, Pallas kernels, body(): pl.pallas_call(functools.partial(kernel, slots), out_shape=(jax.ShapeDtyp...  41.8 us
    pallas_call x1, Pallas kernels, body(): pl.pallas_call(deliver_kernel, out_shape=(jax.ShapeDtypeStruct(field.shap...  2.55 us

profile of v8, /device:TPU:0, one launch (start us, length us, event | category | flops | bytes accessed | tf_op | source)
XLA Modules:
  0.0 45.0 jit_solution(3475598940752613194)
XLA Ops:
  0.6 41.8 %steps.1 = (f32[24,1,128]{2,1,0:T(1,128)}, f32[128,24,128]{2,1,0:T(8,128)}, f32[8,24,128]{2,1,0:T(8,128)}, f32[64,128]{1,0:T(8,128)}, f32[64,128]{1,0:T(8,128)}, /*index=5*/s32[2,1,128]{2,1,0:T(1,128)}) custom-call(f32[24,1,128]{2,1,0:T(1,128)} %les_hbm.1, f32[128,24,128]{2,1,0:T(8,128)} %bitcast.8, s32[2,128]{1,0:T(2,128)} %bitcast.9, s32[2,128]{1,0:T(2,128)} %bitcast.10, ...), custom_call_target="tpu_custom_call" | custom-call | tf_op jit(solution)/shard_map/steps/pallas_call | solution.py:708
  42.4 2.6 %deliver.1 = (f32[24,1,128]{2,1,0:T(1,128)}, f32[128,24,128]{2,1,0:T(8,128)}) custom-call(f32[24,1,128]{2,1,0:T(1,128)} %get-tuple-element.10.les_in, f32[128,24,128]{2,1,0:T(8,128)} %get-tuple-element.11.lines_in, f32[8,24,128]{2,1,0:T(8,128)} %get-tuple-element.12.tiles_in, f32[64,128]{1,0:T(8,128)} %get-tuple-element.13.mask_in, ...), custom_call_target="tpu_custom_call" | custom-call | tf_op jit(solution)/shard_map/deliver/pallas_call | solution.py:782
